TPU v7x, 16 devices: a whole 2x2x2 slice. The times are simulated.
16 devices in a mesh: data: 4 (over z, y), stage: 4 (over x, core).
Axes of the slice: x: 2, y: 2, z: 2, core: 2. Of those that a mesh axis runs over, the one named last changes fastest.
Arguments:
- w_in: float32 [4, 768, 3072], P('stage')
- w_out: float32 [4, 3072, 768], P('stage')
- mom_in: float32 [4, 768, 3072], P('stage')
- mom_out: float32 [4, 3072, 768], P('stage')
- var_in: float32 [4, 768, 3072], P('stage')
- var_out: float32 [4, 3072, 768], P('stage')
- acc_in: float32 [4, 4, 768, 3072], P('data', 'stage')
- acc_out: float32 [4, 4, 3072, 768], P('data', 'stage')
- stage_acts: bfloat16 [4, 8192, 768], P('stage', 'data')
- d_out: bfloat16 [8192, 768], P('data')
- next_x: bfloat16 [16, 8192, 768], P(None, 'data')
- learn_rate: float32 [1], replicated
- max_norm: float32 [1], replicated
Outputs:
- output 1: float32 [4, 768, 3072], P('stage')
- output 2: float32 [4, 3072, 768], P('stage')
- output 3: float32 [4, 768, 3072], P('stage')
- output 4: float32 [4, 3072, 768], P('stage')
- output 5: float32 [4, 768, 3072], P('stage')
- output 6: float32 [4, 3072, 768], P('stage')
- output 7: bfloat16 [16, 8192, 768], P(None, 'data')
All inputs are finite; a program needn't handle non-finite values.
Results may differ from a plain program's by a relative error of at most 0.00652518.
Values are sent between devices in bfloat16 or wider.
A program may use at most 1 GiB of HBM per device.

v0:
```python
import jax
import jax.numpy as jnp
from jax import lax
from jax.sharding import PartitionSpec as P

BETA_ONE = 0.9
BETA_TWO = 0.95
ADAM_EPS = 1e-8
WEIGHT_DECAY = 0.1
STEP_COUNT = 10
NORM_EPS = 1e-6
TRANS_DIMS = (((1,), (1,)), ((), ()))
FIRST_DIMS = (((0,), (0,)), ((), ()))


def gelu_tanh(gelu_in):
    return jax.nn.gelu(gelu_in, approximate=True)


def block_forward(row_block, w_first, w_second):
    hidden = jnp.dot(row_block, w_first, preferred_element_type=jnp.float32)
    act_h = gelu_tanh(hidden).astype(jnp.bfloat16)
    branch = jnp.dot(act_h, w_second, preferred_element_type=jnp.float32)
    return (row_block.astype(jnp.float32) + branch).astype(jnp.bfloat16)


def adamw_update(param_old, moment, second, grad_val, clip_coef, lr_value):
    scaled = clip_coef * grad_val
    mom_new = BETA_ONE * moment + (1.0 - BETA_ONE) * scaled
    sec_new = BETA_TWO * second + (1.0 - BETA_TWO) * scaled * scaled
    mom_hat = mom_new / (1.0 - BETA_ONE ** STEP_COUNT)
    sec_hat = sec_new / (1.0 - BETA_TWO ** STEP_COUNT)
    param_new = param_old - lr_value * (mom_hat / (jnp.sqrt(sec_hat) + ADAM_EPS) + WEIGHT_DECAY * param_old)
    return param_new, mom_new, sec_new


def solution(mesh):
    n_stage = mesh.shape['stage']
    n_rep = mesh.shape['data']
    last_stage = n_stage - 1
    back_perm = [(src, src - 1) for src in range(1, n_stage)]
    fwd_perm = [(src, src + 1) for src in range(last_stage)]
    w_spec = P('stage', None, None)
    acc_spec = P('data', 'stage', None, None)
    row_spec = P(None, 'data', None)

    def stage_program(w_in, w_out, mom_in, mom_out, var_in, var_out, acc_in, acc_out, stage_acts, d_out, next_x, learn_rate, max_norm):
        stage_idx = lax.axis_index('stage')
        w_first = w_in[0].astype(jnp.bfloat16)
        w_second = w_out[0].astype(jnp.bfloat16)
        stage_in = stage_acts[0]
        pre_act = jnp.dot(stage_in, w_first, preferred_element_type=jnp.float32)
        act_h, gelu_vjp = jax.vjp(gelu_tanh, pre_act)
        act_h = act_h.astype(jnp.bfloat16)

        def run_active(operands):
            grad_val = operands[0]
            d_hid = lax.dot_general(grad_val, w_second, TRANS_DIMS, preferred_element_type=jnp.float32)
            d_pre = gelu_vjp(d_hid)[0].astype(jnp.bfloat16)
            d_in = grad_val.astype(jnp.float32) + lax.dot_general(d_pre, w_first, TRANS_DIMS, preferred_element_type=jnp.float32)
            return d_in.astype(jnp.bfloat16), grad_val, d_pre

        def back_step(step_idx, loop_carry):
            return lax.cond(stage_idx == last_stage - step_idx, run_active, lambda operands: operands, loop_carry)

        def back_body(step_idx, loop_carry):
            sent_buf, grad_keep, pre_keep = back_step(step_idx, loop_carry)
            return lax.ppermute(sent_buf, 'stage', back_perm), grad_keep, pre_keep

        init_carry = (d_out, jnp.zeros_like(d_out), jnp.zeros((stage_in.shape[0], w_first.shape[1]), jnp.bfloat16))
        back_carry = lax.fori_loop(0, last_stage, back_body, init_carry)
        _, grad_keep, pre_keep = back_step(last_stage, back_carry)
        dw_first = lax.dot_general(stage_in, pre_keep, FIRST_DIMS, preferred_element_type=jnp.float32)
        dw_second = lax.dot_general(act_h, grad_keep, FIRST_DIMS, preferred_element_type=jnp.float32)
        grad_first = lax.psum(acc_in[0, 0] + dw_first, 'data') / n_rep
        grad_second = lax.psum(acc_out[0, 0] + dw_second, 'data') / n_rep
        part_sq = jnp.sum(grad_first * grad_first) + jnp.sum(grad_second * grad_second)
        total_norm = jnp.sqrt(lax.psum(part_sq, 'stage'))
        clip_coef = jnp.minimum(1.0, max_norm[0] / (total_norm + NORM_EPS))
        new_first, mom_first, sec_first = adamw_update(w_in[0], mom_in[0], var_in[0], grad_first, clip_coef, learn_rate[0])
        new_second, mom_second, sec_second = adamw_update(w_out[0], mom_out[0], var_out[0], grad_second, clip_coef, learn_rate[0])
        fw_first = new_first.astype(jnp.bfloat16)
        fw_second = new_second.astype(jnp.bfloat16)
        n_micro = next_x.shape[0]

        def fwd_step(tick_idx, recv_buf, out_buf):
            micro_idx = tick_idx - stage_idx
            is_valid = (micro_idx >= 0) & (micro_idx < n_micro)
            safe_idx = jnp.clip(micro_idx, 0, n_micro - 1)
            first_in = lax.dynamic_index_in_dim(next_x, safe_idx, 0, keepdims=False)
            row_block = jnp.where(stage_idx == 0, first_in, recv_buf)
            result = lax.cond(is_valid, lambda rows_in: block_forward(rows_in, fw_first, fw_second), lambda rows_in: rows_in, row_block)
            old_slice = lax.dynamic_index_in_dim(out_buf, safe_idx, 0, keepdims=False)
            new_slice = jnp.where(is_valid & (stage_idx == last_stage), result, old_slice)
            return result, lax.dynamic_update_index_in_dim(out_buf, new_slice, safe_idx, 0)

        def fwd_body(tick_idx, loop_carry):
            result, out_buf = fwd_step(tick_idx, loop_carry[0], loop_carry[1])
            return lax.ppermute(result, 'stage', fwd_perm), out_buf

        n_ticks = n_stage + n_micro - 1
        fwd_carry = lax.fori_loop(0, n_ticks - 1, fwd_body, (jnp.zeros_like(next_x[0]), jnp.zeros_like(next_x)))
        _, out_buf = fwd_step(n_ticks - 1, fwd_carry[0], fwd_carry[1])
        next_y = lax.psum(jnp.where(stage_idx == last_stage, out_buf, jnp.zeros_like(out_buf)), 'stage')
        return (new_first[None], new_second[None], mom_first[None], mom_second[None], sec_first[None], sec_second[None], next_y)

    return jax.shard_map(stage_program, mesh=mesh, in_specs=(w_spec, w_spec, w_spec, w_spec, w_spec, w_spec, acc_spec, acc_spec, P('stage', 'data', None), P('data', None), row_spec, P(None), P(None)), out_specs=(w_spec, w_spec, w_spec, w_spec, w_spec, w_spec, row_spec), check_vma=False)
```

profile of v0, /device:TPU:0, one launch (start us, length us, event | category | flops | bytes accessed | tf_op | source)
XLA Modules:
  0.0 2965.0 jit_solution(17166800240927186135)
XLA Ops:
  20.7 38.2 %multiply_multiply_fusion.2 = (f32[2048,3072]{1,0:T(8,128)}, f32[2048,3072]{1,0:T(8,128)}, f32[2048,3072]{1,0:T(8,128)}, f32[2048,3072]{1,0:T(8,128)}) fusion(f32[1,768,3072]{2,1,0:T(8,128)} %param.25, bf16[1,2048,768]{2,1,0:T(8,128)(2,1)S(1)} %copy-done), kind=kOutput, calls=%fused_computation.40 | convolution fusion | flops 9728950272 | bytes 113246208 | tf_op jit(solution)/shard_map/dot_general | solution.py:52
  86.1 234.9 %while.33 = (s32[]{:T(128)}, bf16[2048,768]{1,0:T(8,128)(2,1)}, bf16[2048,768]{1,0:T(8,128)(2,1)}, bf16[2048,3072]{1,0:T(8,128)(2,1)}, s32[]{:T(128)}, /*index=5...) while((s32[]{:T(128)}, bf16[2048,768]{1,0:T(8,128)(2,1)}, ...), condition=%wide.region_3.0_spmd, body=%wide.region_0.0_spmd.sunk | while | flops 19394985984 | bytes 163578160 | solution.py:71
  102.9 38.1 %collective-permute-done = bf16[2048,768]{1,0:T(8,128)(2,1)} collective-permute-done((bf16[2048,768]{1,0:T(8,128)(2,1)}, bf16[2048,768]{1,0:T(8,128)(2,1)}, u32[]{:S(2)}, u32[]{:S(2)}) %collective-permute-start) | collective-permute-done | bytes 3145760 | tf_op jit(solution)/shard_map/while/body/eval_jaxpr/ppermute | solution.py:68
  146.1 175.0 %collective-permute-done = bf16[2048,768]{1,0:T(8,128)(2,1)} collective-permute-done((bf16[2048,768]{1,0:T(8,128)(2,1)}, bf16[2048,768]{1,0:T(8,128)(2,1)}, u32[]{:S(2)}, u32[]{:S(2)}) %collective-permute-start) | collective-permute-done | bytes 3145760 | tf_op jit(solution)/shard_map/while/body/eval_jaxpr/ppermute | solution.py:68
  330.6 44.5 %conditional.4 = ((bf16[2048,768]{1,0:T(8,128)(2,1)}, bf16[2048,3072]{1,0:T(8,128)(2,1)})) conditional(s32[]{:T(128)} %convert_element_type.71, (bf16[2048,768]{1,0:T(8,128)(2,1)}, bf16[2048,3072]{1,0:T(8,128)(2,1)}) %tuple.72, (bf16[2048,768]{1,0:T(8,128)(2,1)}, bf16[3072,768]{1,0:T(8,128)(2,1)}, f32[2048,3072]{1,0:T(8,128)}, ...), branch_computations={%region_4.0_spmd, %region_5.0_spmd} | conditional | flops 9726590976 | bytes 127402008 | solution.py:64
  330.6 40.8 %add_convert_fusion.2 = bf16[2048,3072]{1,0:T(8,128)(2,1)} fusion(f32[2048,3072]{1,0:T(8,128)} %get-tuple-element.412, f32[2048,3072]{1,0:T(8,128)} %get-tuple-element.411, f32[2048,3072]{1,0:T(8,128)} %get-tuple-element.410, f32[2048,3072]{1,0:T(8,128)} %get-tuple-element.409, bf16[2048,768]{1,0:T(8,128)(2,1)} %get-tuple-element.709, ...), kind=kOutput, calls=%fused_computation.2 | convolution fusion | flops 9726590976 | bytes 121110528 | tf_op jit(solution)/shard_map/cond/branch_1_fun/dot_general | solution.py:58
  435.8 313.3 %all-reduce.6.cloned.1.call-done = (f32[768,3072]{0,1:T(8,128)}, f32[3072,768]{1,0:T(8,128)}) async-done(((f32[768,3072]{0,1:T(8,128)}, f32[3072,768]{1,0:T(8,128)}), (f32[768,3072]{0,1:T(8,128)}, f32[3072,768]{1,0:T(8,128)})) %all-reduce.6.cloned.1.call-update) | async-done | bytes 18874384 | tf_op jit(solution)/shard_map/psum | solution.py:75
  849.5 1148.8 %while.34 = (s32[]{:T(128)}, bf16[2048,768]{1,0:T(8,128)(2,1)}, bf16[16,2048,768]{2,1,0:T(8,128)(2,1)}, s32[]{:T(128)}, pred[]{:T(512)}, /*index=5*/bf16[16,2048...) while((s32[]{:T(128)}, bf16[2048,768]{1,0:T(8,128)(2,1)}, ...), condition=%wide.region_14.15_spmd, body=%wide.region_11.14_spmd.sunk | while | flops 19391840256 | bytes 59769108 | solution.py:102
  1023.9 34.9 %collective-permute-start.1 = (bf16[2048,768]{1,0:T(8,128)(2,1)S(1)}, bf16[2048,768]{1,0:T(8,128)(2,1)}, u32[]{:S(2)}, u32[]{:S(2)}) collective-permute-start(bf16[2048,768]{1,0:T(8,128)(2,1)S(1)} %get-tuple-element.761), channel_id=1, source_target_pairs={{0,1},{1,2},{2,3},{4,5},{5,6},{6,7},{8,9},{9,10},{10,11},{12,13},{... | collective-permute-start | bytes 9437192 | tf_op jit(solution)/shard_map/while/body/eval_jaxpr/ppermute | solution.py:99
  1092.6 34.9 %collective-permute-start.1 = (bf16[2048,768]{1,0:T(8,128)(2,1)S(1)}, bf16[2048,768]{1,0:T(8,128)(2,1)}, u32[]{:S(2)}, u32[]{:S(2)}) collective-permute-start(bf16[2048,768]{1,0:T(8,128)(2,1)S(1)} %get-tuple-element.761), channel_id=1, source_target_pairs={{0,1},{1,2},{2,3},{4,5},{5,6},{6,7},{8,9},{9,10},{10,11},{12,13},{... | collective-permute-start | bytes 9437192 | tf_op jit(solution)/shard_map/while/body/eval_jaxpr/ppermute | solution.py:99
  1161.3 34.9 %collective-permute-start.1 = (bf16[2048,768]{1,0:T(8,128)(2,1)S(1)}, bf16[2048,768]{1,0:T(8,128)(2,1)}, u32[]{:S(2)}, u32[]{:S(2)}) collective-permute-start(bf16[2048,768]{1,0:T(8,128)(2,1)S(1)} %get-tuple-element.761), channel_id=1, source_target_pairs={{0,1},{1,2},{2,3},{4,5},{5,6},{6,7},{8,9},{9,10},{10,11},{12,13},{... | collective-permute-start | bytes 9437192 | tf_op jit(solution)/shard_map/while/body/eval_jaxpr/ppermute | solution.py:99
  1230.0 34.9 %collective-permute-start.1 = (bf16[2048,768]{1,0:T(8,128)(2,1)S(1)}, bf16[2048,768]{1,0:T(8,128)(2,1)}, u32[]{:S(2)}, u32[]{:S(2)}) collective-permute-start(bf16[2048,768]{1,0:T(8,128)(2,1)S(1)} %get-tuple-element.761), channel_id=1, source_target_pairs={{0,1},{1,2},{2,3},{4,5},{5,6},{6,7},{8,9},{9,10},{10,11},{12,13},{... | collective-permute-start | bytes 9437192 | tf_op jit(solution)/shard_map/while/body/eval_jaxpr/ppermute | solution.py:99
  1298.7 34.9 %collective-permute-start.1 = (bf16[2048,768]{1,0:T(8,128)(2,1)S(1)}, bf16[2048,768]{1,0:T(8,128)(2,1)}, u32[]{:S(2)}, u32[]{:S(2)}) collective-permute-start(bf16[2048,768]{1,0:T(8,128)(2,1)S(1)} %get-tuple-element.761), channel_id=1, source_target_pairs={{0,1},{1,2},{2,3},{4,5},{5,6},{6,7},{8,9},{9,10},{10,11},{12,13},{... | collective-permute-start | bytes 9437192 | tf_op jit(solution)/shard_map/while/body/eval_jaxpr/ppermute | solution.py:99
  1367.4 34.9 %collective-permute-start.1 = (bf16[2048,768]{1,0:T(8,128)(2,1)S(1)}, bf16[2048,768]{1,0:T(8,128)(2,1)}, u32[]{:S(2)}, u32[]{:S(2)}) collective-permute-start(bf16[2048,768]{1,0:T(8,128)(2,1)S(1)} %get-tuple-element.761), channel_id=1, source_target_pairs={{0,1},{1,2},{2,3},{4,5},{5,6},{6,7},{8,9},{9,10},{10,11},{12,13},{... | collective-permute-start | bytes 9437192 | tf_op jit(solution)/shard_map/while/body/eval_jaxpr/ppermute | solution.py:99
  1436.1 34.9 %collective-permute-start.1 = (bf16[2048,768]{1,0:T(8,128)(2,1)S(1)}, bf16[2048,768]{1,0:T(8,128)(2,1)}, u32[]{:S(2)}, u32[]{:S(2)}) collective-permute-start(bf16[2048,768]{1,0:T(8,128)(2,1)S(1)} %get-tuple-element.761), channel_id=1, source_target_pairs={{0,1},{1,2},{2,3},{4,5},{5,6},{6,7},{8,9},{9,10},{10,11},{12,13},{... | collective-permute-start | bytes 9437192 | tf_op jit(solution)/shard_map/while/body/eval_jaxpr/ppermute | solution.py:99
  1504.8 34.9 %collective-permute-start.1 = (bf16[2048,768]{1,0:T(8,128)(2,1)S(1)}, bf16[2048,768]{1,0:T(8,128)(2,1)}, u32[]{:S(2)}, u32[]{:S(2)}) collective-permute-start(bf16[2048,768]{1,0:T(8,128)(2,1)S(1)} %get-tuple-element.761), channel_id=1, source_target_pairs={{0,1},{1,2},{2,3},{4,5},{5,6},{6,7},{8,9},{9,10},{10,11},{12,13},{... | collective-permute-start | bytes 9437192 | tf_op jit(solution)/shard_map/while/body/eval_jaxpr/ppermute | solution.py:99
  1573.5 34.9 %collective-permute-start.1 = (bf16[2048,768]{1,0:T(8,128)(2,1)S(1)}, bf16[2048,768]{1,0:T(8,128)(2,1)}, u32[]{:S(2)}, u32[]{:S(2)}) collective-permute-start(bf16[2048,768]{1,0:T(8,128)(2,1)S(1)} %get-tuple-element.761), channel_id=1, source_target_pairs={{0,1},{1,2},{2,3},{4,5},{5,6},{6,7},{8,9},{9,10},{10,11},{12,13},{... | collective-permute-start | bytes 9437192 | tf_op jit(solution)/shard_map/while/body/eval_jaxpr/ppermute | solution.py:99
  1642.2 34.9 %collective-permute-start.1 = (bf16[2048,768]{1,0:T(8,128)(2,1)S(1)}, bf16[2048,768]{1,0:T(8,128)(2,1)}, u32[]{:S(2)}, u32[]{:S(2)}) collective-permute-start(bf16[2048,768]{1,0:T(8,128)(2,1)S(1)} %get-tuple-element.761), channel_id=1, source_target_pairs={{0,1},{1,2},{2,3},{4,5},{5,6},{6,7},{8,9},{9,10},{10,11},{12,13},{... | collective-permute-start | bytes 9437192 | tf_op jit(solution)/shard_map/while/body/eval_jaxpr/ppermute | solution.py:99
  1710.9 34.9 %collective-permute-start.1 = (bf16[2048,768]{1,0:T(8,128)(2,1)S(1)}, bf16[2048,768]{1,0:T(8,128)(2,1)}, u32[]{:S(2)}, u32[]{:S(2)}) collective-permute-start(bf16[2048,768]{1,0:T(8,128)(2,1)S(1)} %get-tuple-element.761), channel_id=1, source_target_pairs={{0,1},{1,2},{2,3},{4,5},{5,6},{6,7},{8,9},{9,10},{10,11},{12,13},{... | collective-permute-start | bytes 9437192 | tf_op jit(solution)/shard_map/while/body/eval_jaxpr/ppermute | solution.py:99
  1779.6 34.9 %collective-permute-start.1 = (bf16[2048,768]{1,0:T(8,128)(2,1)S(1)}, bf16[2048,768]{1,0:T(8,128)(2,1)}, u32[]{:S(2)}, u32[]{:S(2)}) collective-permute-start(bf16[2048,768]{1,0:T(8,128)(2,1)S(1)} %get-tuple-element.761), channel_id=1, source_target_pairs={{0,1},{1,2},{2,3},{4,5},{5,6},{6,7},{8,9},{9,10},{10,11},{12,13},{... | collective-permute-start | bytes 9437192 | tf_op jit(solution)/shard_map/while/body/eval_jaxpr/ppermute | solution.py:99
  1848.3 34.9 %collective-permute-start.1 = (bf16[2048,768]{1,0:T(8,128)(2,1)S(1)}, bf16[2048,768]{1,0:T(8,128)(2,1)}, u32[]{:S(2)}, u32[]{:S(2)}) collective-permute-start(bf16[2048,768]{1,0:T(8,128)(2,1)S(1)} %get-tuple-element.761), channel_id=1, source_target_pairs={{0,1},{1,2},{2,3},{4,5},{5,6},{6,7},{8,9},{9,10},{10,11},{12,13},{... | collective-permute-start | bytes 9437192 | tf_op jit(solution)/shard_map/while/body/eval_jaxpr/ppermute | solution.py:99
  1890.1 61.8 %collective-permute-start.1 = (bf16[2048,768]{1,0:T(8,128)(2,1)S(1)}, bf16[2048,768]{1,0:T(8,128)(2,1)}, u32[]{:S(2)}, u32[]{:S(2)}) collective-permute-start(bf16[2048,768]{1,0:T(8,128)(2,1)S(1)} %get-tuple-element.761), channel_id=1, source_target_pairs={{0,1},{1,2},{2,3},{4,5},{5,6},{6,7},{8,9},{9,10},{10,11},{12,13},{... | collective-permute-start | bytes 9437192 | tf_op jit(solution)/shard_map/while/body/eval_jaxpr/ppermute | solution.py:99
  1958.8 34.9 %collective-permute-start.1 = (bf16[2048,768]{1,0:T(8,128)(2,1)S(1)}, bf16[2048,768]{1,0:T(8,128)(2,1)}, u32[]{:S(2)}, u32[]{:S(2)}) collective-permute-start(bf16[2048,768]{1,0:T(8,128)(2,1)S(1)} %get-tuple-element.761), channel_id=1, source_target_pairs={{0,1},{1,2},{2,3},{4,5},{5,6},{6,7},{8,9},{9,10},{10,11},{12,13},{... | collective-permute-start | bytes 9437192 | tf_op jit(solution)/shard_map/while/body/eval_jaxpr/ppermute | solution.py:99
  2053.6 869.9 %all-reduce.4.cloned.1.call-done = bf16[16,2048,768]{2,1,0:T(8,128)(2,1)} async-done(((bf16[16,2048,768]{2,1,0:T(8,128)(2,1)}), bf16[16,2048,768]{2,1,0:T(8,128)(2,1)}) %all-reduce.4.cloned.1.call-update) | async-done | bytes 50331664 | tf_op jit(solution)/shard_map/psum | solution.py:104
  (175 shorter events, 1362.8 us)
Async XLA Ops:
  7.2 742.0 %all-reduce.6.cloned.1.call-start = ((), (), s32[]{:S(2)}) async-start(), calls=%async_computation.1 | async-start | bytes 37748736 | tf_op jit(solution)/shard_map/psum | solution.py:75
  90.1 7.7 collective-permute-start
  101.6 39.4 %collective-permute-start = (bf16[2048,768]{1,0:T(8,128)(2,1)}, bf16[2048,768]{1,0:T(8,128)(2,1)}, u32[]{:S(2)}, u32[]{:S(2)}) collective-permute-start(bf16[2048,768]{1,0:T(8,128)(2,1)} %get-tuple-element.650), channel_id=1, source_target_pairs={{1,0},{2,1},{3,2},{5,4},{6,5},{7,6},{9,8},{10,9},{11,10},{13,12},{... | collective-permute-start | bytes 9437192 | tf_op jit(solution)/shard_map/while/body/eval_jaxpr/ppermute | solution.py:68
  144.8 176.3 %collective-permute-start = (bf16[2048,768]{1,0:T(8,128)(2,1)}, bf16[2048,768]{1,0:T(8,128)(2,1)}, u32[]{:S(2)}, u32[]{:S(2)}) collective-permute-start(bf16[2048,768]{1,0:T(8,128)(2,1)} %get-tuple-element.650), channel_id=1, source_target_pairs={{1,0},{2,1},{3,2},{5,4},{6,5},{7,6},{9,8},{10,9},{11,10},{13,12},{... | collective-permute-start | bytes 9437192 | tf_op jit(solution)/shard_map/while/body/eval_jaxpr/ppermute | solution.py:68
  415.1 2508.4 %all-reduce.4.cloned.1.call-start = ((), (), s32[]{:S(2)}) async-start(), calls=%async_computation | async-start | bytes 100663296 | tf_op jit(solution)/shard_map/psum | solution.py:104
  878.9 7.6 collective-permute-start.1
  915.6 12.9 collective-permute-start.1
  957.7 37.1 %collective-permute-start.1 = (bf16[2048,768]{1,0:T(8,128)(2,1)S(1)}, bf16[2048,768]{1,0:T(8,128)(2,1)}, u32[]{:S(2)}, u32[]{:S(2)}) collective-permute-start(bf16[2048,768]{1,0:T(8,128)(2,1)S(1)} %get-tuple-element.761), channel_id=1, source_target_pairs={{0,1},{1,2},{2,3},{4,5},{5,6},{6,7},{8,9},{9,10},{10,11},{12,13},{... | collective-permute-start | bytes 9437192 | tf_op jit(solution)/shard_map/while/body/eval_jaxpr/ppermute | solution.py:99
  1023.9 39.5 %collective-permute-start.1 = (bf16[2048,768]{1,0:T(8,128)(2,1)S(1)}, bf16[2048,768]{1,0:T(8,128)(2,1)}, u32[]{:S(2)}, u32[]{:S(2)}) collective-permute-start(bf16[2048,768]{1,0:T(8,128)(2,1)S(1)} %get-tuple-element.761), channel_id=1, source_target_pairs={{0,1},{1,2},{2,3},{4,5},{5,6},{6,7},{8,9},{9,10},{10,11},{12,13},{... | collective-permute-start | bytes 9437192 | tf_op jit(solution)/shard_map/while/body/eval_jaxpr/ppermute | solution.py:99
  1092.6 39.5 %collective-permute-start.1 = (bf16[2048,768]{1,0:T(8,128)(2,1)S(1)}, bf16[2048,768]{1,0:T(8,128)(2,1)}, u32[]{:S(2)}, u32[]{:S(2)}) collective-permute-start(bf16[2048,768]{1,0:T(8,128)(2,1)S(1)} %get-tuple-element.761), channel_id=1, source_target_pairs={{0,1},{1,2},{2,3},{4,5},{5,6},{6,7},{8,9},{9,10},{10,11},{12,13},{... | collective-permute-start | bytes 9437192 | tf_op jit(solution)/shard_map/while/body/eval_jaxpr/ppermute | solution.py:99
  1161.3 39.5 %collective-permute-start.1 = (bf16[2048,768]{1,0:T(8,128)(2,1)S(1)}, bf16[2048,768]{1,0:T(8,128)(2,1)}, u32[]{:S(2)}, u32[]{:S(2)}) collective-permute-start(bf16[2048,768]{1,0:T(8,128)(2,1)S(1)} %get-tuple-element.761), channel_id=1, source_target_pairs={{0,1},{1,2},{2,3},{4,5},{5,6},{6,7},{8,9},{9,10},{10,11},{12,13},{... | collective-permute-start | bytes 9437192 | tf_op jit(solution)/shard_map/while/body/eval_jaxpr/ppermute | solution.py:99
  1230.0 39.5 %collective-permute-start.1 = (bf16[2048,768]{1,0:T(8,128)(2,1)S(1)}, bf16[2048,768]{1,0:T(8,128)(2,1)}, u32[]{:S(2)}, u32[]{:S(2)}) collective-permute-start(bf16[2048,768]{1,0:T(8,128)(2,1)S(1)} %get-tuple-element.761), channel_id=1, source_target_pairs={{0,1},{1,2},{2,3},{4,5},{5,6},{6,7},{8,9},{9,10},{10,11},{12,13},{... | collective-permute-start | bytes 9437192 | tf_op jit(solution)/shard_map/while/body/eval_jaxpr/ppermute | solution.py:99
  1298.7 39.5 %collective-permute-start.1 = (bf16[2048,768]{1,0:T(8,128)(2,1)S(1)}, bf16[2048,768]{1,0:T(8,128)(2,1)}, u32[]{:S(2)}, u32[]{:S(2)}) collective-permute-start(bf16[2048,768]{1,0:T(8,128)(2,1)S(1)} %get-tuple-element.761), channel_id=1, source_target_pairs={{0,1},{1,2},{2,3},{4,5},{5,6},{6,7},{8,9},{9,10},{10,11},{12,13},{... | collective-permute-start | bytes 9437192 | tf_op jit(solution)/shard_map/while/body/eval_jaxpr/ppermute | solution.py:99
  1367.4 39.5 %collective-permute-start.1 = (bf16[2048,768]{1,0:T(8,128)(2,1)S(1)}, bf16[2048,768]{1,0:T(8,128)(2,1)}, u32[]{:S(2)}, u32[]{:S(2)}) collective-permute-start(bf16[2048,768]{1,0:T(8,128)(2,1)S(1)} %get-tuple-element.761), channel_id=1, source_target_pairs={{0,1},{1,2},{2,3},{4,5},{5,6},{6,7},{8,9},{9,10},{10,11},{12,13},{... | collective-permute-start | bytes 9437192 | tf_op jit(solution)/shard_map/while/body/eval_jaxpr/ppermute | solution.py:99
  1436.1 39.5 %collective-permute-start.1 = (bf16[2048,768]{1,0:T(8,128)(2,1)S(1)}, bf16[2048,768]{1,0:T(8,128)(2,1)}, u32[]{:S(2)}, u32[]{:S(2)}) collective-permute-start(bf16[2048,768]{1,0:T(8,128)(2,1)S(1)} %get-tuple-element.761), channel_id=1, source_target_pairs={{0,1},{1,2},{2,3},{4,5},{5,6},{6,7},{8,9},{9,10},{10,11},{12,13},{... | collective-permute-start | bytes 9437192 | tf_op jit(solution)/shard_map/while/body/eval_jaxpr/ppermute | solution.py:99
  1504.8 39.5 %collective-permute-start.1 = (bf16[2048,768]{1,0:T(8,128)(2,1)S(1)}, bf16[2048,768]{1,0:T(8,128)(2,1)}, u32[]{:S(2)}, u32[]{:S(2)}) collective-permute-start(bf16[2048,768]{1,0:T(8,128)(2,1)S(1)} %get-tuple-element.761), channel_id=1, source_target_pairs={{0,1},{1,2},{2,3},{4,5},{5,6},{6,7},{8,9},{9,10},{10,11},{12,13},{... | collective-permute-start | bytes 9437192 | tf_op jit(solution)/shard_map/while/body/eval_jaxpr/ppermute | solution.py:99
  1573.5 39.5 %collective-permute-start.1 = (bf16[2048,768]{1,0:T(8,128)(2,1)S(1)}, bf16[2048,768]{1,0:T(8,128)(2,1)}, u32[]{:S(2)}, u32[]{:S(2)}) collective-permute-start(bf16[2048,768]{1,0:T(8,128)(2,1)S(1)} %get-tuple-element.761), channel_id=1, source_target_pairs={{0,1},{1,2},{2,3},{4,5},{5,6},{6,7},{8,9},{9,10},{10,11},{12,13},{... | collective-permute-start | bytes 9437192 | tf_op jit(solution)/shard_map/while/body/eval_jaxpr/ppermute | solution.py:99
  1642.2 39.5 %collective-permute-start.1 = (bf16[2048,768]{1,0:T(8,128)(2,1)S(1)}, bf16[2048,768]{1,0:T(8,128)(2,1)}, u32[]{:S(2)}, u32[]{:S(2)}) collective-permute-start(bf16[2048,768]{1,0:T(8,128)(2,1)S(1)} %get-tuple-element.761), channel_id=1, source_target_pairs={{0,1},{1,2},{2,3},{4,5},{5,6},{6,7},{8,9},{9,10},{10,11},{12,13},{... | collective-permute-start | bytes 9437192 | tf_op jit(solution)/shard_map/while/body/eval_jaxpr/ppermute | solution.py:99
  1710.9 39.5 %collective-permute-start.1 = (bf16[2048,768]{1,0:T(8,128)(2,1)S(1)}, bf16[2048,768]{1,0:T(8,128)(2,1)}, u32[]{:S(2)}, u32[]{:S(2)}) collective-permute-start(bf16[2048,768]{1,0:T(8,128)(2,1)S(1)} %get-tuple-element.761), channel_id=1, source_target_pairs={{0,1},{1,2},{2,3},{4,5},{5,6},{6,7},{8,9},{9,10},{10,11},{12,13},{... | collective-permute-start | bytes 9437192 | tf_op jit(solution)/shard_map/while/body/eval_jaxpr/ppermute | solution.py:99
  1779.6 39.5 %collective-permute-start.1 = (bf16[2048,768]{1,0:T(8,128)(2,1)S(1)}, bf16[2048,768]{1,0:T(8,128)(2,1)}, u32[]{:S(2)}, u32[]{:S(2)}) collective-permute-start(bf16[2048,768]{1,0:T(8,128)(2,1)S(1)} %get-tuple-element.761), channel_id=1, source_target_pairs={{0,1},{1,2},{2,3},{4,5},{5,6},{6,7},{8,9},{9,10},{10,11},{12,13},{... | collective-permute-start | bytes 9437192 | tf_op jit(solution)/shard_map/while/body/eval_jaxpr/ppermute | solution.py:99
  1848.3 39.5 %collective-permute-start.1 = (bf16[2048,768]{1,0:T(8,128)(2,1)S(1)}, bf16[2048,768]{1,0:T(8,128)(2,1)}, u32[]{:S(2)}, u32[]{:S(2)}) collective-permute-start(bf16[2048,768]{1,0:T(8,128)(2,1)S(1)} %get-tuple-element.761), channel_id=1, source_target_pairs={{0,1},{1,2},{2,3},{4,5},{5,6},{6,7},{8,9},{9,10},{10,11},{12,13},{... | collective-permute-start | bytes 9437192 | tf_op jit(solution)/shard_map/while/body/eval_jaxpr/ppermute | solution.py:99
  1890.1 66.5 %collective-permute-start.1 = (bf16[2048,768]{1,0:T(8,128)(2,1)S(1)}, bf16[2048,768]{1,0:T(8,128)(2,1)}, u32[]{:S(2)}, u32[]{:S(2)}) collective-permute-start(bf16[2048,768]{1,0:T(8,128)(2,1)S(1)} %get-tuple-element.761), channel_id=1, source_target_pairs={{0,1},{1,2},{2,3},{4,5},{5,6},{6,7},{8,9},{9,10},{10,11},{12,13},{... | collective-permute-start | bytes 9437192 | tf_op jit(solution)/shard_map/while/body/eval_jaxpr/ppermute | solution.py:99
  1958.8 39.5 %collective-permute-start.1 = (bf16[2048,768]{1,0:T(8,128)(2,1)S(1)}, bf16[2048,768]{1,0:T(8,128)(2,1)}, u32[]{:S(2)}, u32[]{:S(2)}) collective-permute-start(bf16[2048,768]{1,0:T(8,128)(2,1)S(1)} %get-tuple-element.761), channel_id=1, source_target_pairs={{0,1},{1,2},{2,3},{4,5},{5,6},{6,7},{8,9},{9,10},{10,11},{12,13},{... | collective-permute-start | bytes 9437192 | tf_op jit(solution)/shard_map/while/body/eval_jaxpr/ppermute | solution.py:99
  2923.5 34.3 %copy-start.1 = (bf16[1,2048,768]{2,1,0:T(8,128)(2,1)S(1)}, bf16[1,2048,768]{2,1,0:T(8,128)(2,1)}, u32[]{:S(2)}) copy-start(bf16[1,2048,768]{2,1,0:T(8,128)(2,1)} %param.33) | copy-start | bytes 9437188
  (2 other events, 20.4 us)
Sparse Core Ops, SparseCore 0:
  415.2 333.8 all-reduce.5
  2025.0 898.4 all-reduce.3
where the time goes:
time: 2970 us
  waiting for transfers between devices  1400 us (47%)
  starting transfers between devices  598 us (20%)
  matrix products  523 us (18%)
  local copies, waits for them, and re-layouts  227 us (8%)
  other arithmetic  188 us (6%)
    psum x1, waiting for transfers between devices, stage_program(): lax.psum(jnp.where(stage_idx == last_stage, out_buf, jnp.zeros_like(out_b...  870 us
    ppermute x18, starting transfers between devices, fwd_body(): return (lax.ppermute(result, 'stage', fwd_perm), out_buf)  594 us
    dot_general x16, matrix products, block_forward(): branch = jnp.dot(act_h, w_second, preferred_element_type=jnp.float32)  404 us
    psum x1, waiting for transfers between devices, stage_program(): grad_first = lax.psum(acc_in[0, 0] + dw_first, 'data') / n_rep  313 us
    ppermute x3, waiting for transfers between devices, back_body(): return (lax.ppermute(sent_buf, 'stage', back_perm), grad_keep, pre_keep)  220 us
    unnamed x15, local copies, waits for them, and re-layouts  105 us
  transfers between devices with their start and end apart: 23, of which 5 were waited for; matrix products, arithmetic and copies ran while one was open for 4% of the time, Pallas kernels for 0%

commit v1 on v0

v1 whole, which is shorter than its diff:
```python
import functools

import jax
import jax.numpy as jnp
from jax import lax
from jax.experimental import pallas as pl
from jax.experimental.pallas import tpu as pltpu
from jax.sharding import PartitionSpec as P

BETA_ONE = 0.9
BETA_TWO = 0.95
ADAM_EPS = 1e-8
WEIGHT_DECAY = 0.1
STEP_COUNT = 10
NORM_EPS = 1e-6
TRANS_DIMS = (((1,), (1,)), ((), ()))
FIRST_DIMS = (((0,), (0,)), ((), ()))
F32 = jnp.float32
BF16 = jnp.bfloat16
TILE = 512
DIM = 768
HALF = 384
FFN = 3072
ROWS = 2048
MIB = 1024 * 1024
ROW_BYTES = 3072
CUBE = 0.044715
ROOT = 0.7978845608
STRIP = 64
VMEM_BIG = 63 * MIB
DMA = pltpu.SemaphoreType.DMA
MESH_ID = pl.DeviceIdType.MESH
ANY = pl.BlockSpec(memory_space=pl.ANY)

STAGES = range(4)
OWN, MATE, FAR, RELAY = STAGES
CORE_PERM = [(s, s ^ MATE) for s in STAGES]
X_PERM = [(s, s ^ FAR) for s in STAGES]
CHUNK_0, CHUNK_1, CHUNK_2 = [(group, 0, ROWS) for group in range(3)]
CHUNK_3, CHUNK_4 = [(3, row, ROWS // 2) for row in (0, ROWS // 2)]
DIAG, SIDE_Y, SIDE_Z, SELF = range(4)
LONG, SHORT, SUMS = range(3)
FIRST, SECOND = range(2)


def gelu_tanh(gelu_in):
    return jax.nn.gelu(gelu_in, approximate=True)


def adamw_update(param_old, moment, second, grad_val, clip_coef, lr_value):
    scaled = clip_coef * grad_val
    mom_new = BETA_ONE * moment + (1.0 - BETA_ONE) * scaled
    sec_new = BETA_TWO * second + (1.0 - BETA_TWO) * scaled * scaled
    mom_hat = mom_new / (1.0 - BETA_ONE ** STEP_COUNT)
    sec_hat = sec_new / (1.0 - BETA_TWO ** STEP_COUNT)
    param_new = param_old - lr_value * (mom_hat / (jnp.sqrt(sec_hat) + ADAM_EPS) + WEIGHT_DECAY * param_old)
    return param_new, mom_new, sec_new


def gelu_kernel(z):
    half = 0.5 * z
    return half + half * jnp.tanh(z * (ROOT + ROOT * CUBE * (z * z)))


def forward_kernel(n_blk, spec, n_side, side_rows, gather, *refs):
    in_next, first_group, row0, n_rows, to_out, has_out_in = spec
    refs = list(refs)
    ends = [sum(k[-1] for k in side_rows[:i]) for i in range(n_side)]
    x_ref = refs.pop(0)
    w_refs = [(refs.pop(0), refs.pop(0)) for _ in range(n_blk)]
    q_ref = refs.pop(0) if gather else None
    side_refs = [refs.pop(0) for _ in range(n_side)]
    if has_out_in:
        refs.pop(0)
    if to_out:
        out_ref = refs.pop(0)
    y_ref = refs.pop(0)
    gathered = [refs.pop(0) for _ in range(2)] if gather else None
    w_buf, x_buf, h_buf, w_sem, x_sem, y_sem, o_sem = refs[:7]
    bounce = refs[7:]
    steps = None
    if gather:
        z_v, m_v = bounce[:2]
        steps = exchange_steps(lambda part: q_ref.at[part], z_v, m_v, bounce[2:9])
    stage = lax.axis_index('stage')
    core = lax.rem(stage, 2)
    n_tiles = n_rows // TILE
    n_mb = max(1, n_rows // ROWS)
    mb_rows = n_rows // n_mb

    def x_copies():
        if not in_next:
            return [pltpu.make_async_copy(x_ref.at[pl.ds(row0, n_rows)], x_buf, x_sem.at[0])]
        return [
            pltpu.make_async_copy(
                x_ref.at[4 * (first_group + q) + stage, pl.ds(row0, mb_rows)],
                x_buf.at[pl.ds(q * mb_rows, mb_rows)], x_sem.at[q])
            for q in range(n_mb)]

    def w_copies(blk):
        own = pl.multiple_of(core * HALF, HALF)
        mate = pl.multiple_of((1 - core) * HALF, HALF)
        return [
            pltpu.make_async_copy(w_refs[blk][0], w_buf.at[blk, :, :, pl.ds(own, HALF)], w_sem.at[blk, 0]),
            pltpu.make_async_copy(w_refs[blk][1], w_buf.at[blk, :, :, pl.ds(mate, HALF)], w_sem.at[blk, 1])]

    for cp in x_copies() + w_copies(0):
        cp.start()
    for cp in x_copies():
        cp.wait()
    if n_side:
        side_buf, si_sem, so_sem = bounce

    def side_in(i):
        return pltpu.make_async_copy(side_refs[i], side_buf.at[pl.ds(ends[i], side_rows[i][-1])], si_sem.at[i])

    def side_out(i):
        flip, group, off, rows = side_rows[i]
        owner = stage if flip == OWN else jnp.bitwise_xor(stage, flip)
        return pltpu.make_async_copy(
            side_buf.at[pl.ds(ends[i], rows)],
            out_ref.at[4 * group + owner, pl.ds(off, rows)], so_sem.at[i])

    def y_copy(t):
        return pltpu.make_async_copy(x_buf.at[pl.ds(pl.multiple_of(t * TILE, TILE), TILE)], y_ref.at[pl.ds(pl.multiple_of(t * TILE, TILE), TILE)], y_sem.at[t])

    def o_copy(t):
        return pltpu.make_async_copy(x_buf.at[pl.ds(pl.multiple_of(t * TILE, TILE), TILE)], out_ref.at[4 * first_group + stage, pl.ds(row0 + pl.multiple_of(t * TILE, TILE), TILE)], o_sem.at[t])

    def blk_body(blk, _):
        for half in range(2):
            pltpu.make_async_copy(w_buf.at[blk, :, :, pl.ds(0, HALF)], w_buf.at[blk, :, :, pl.ds(0, HALF)], w_sem.at[blk, half]).wait()
        for nxt in range(1, n_blk):
            @pl.when(blk == nxt - 1)
            def _():
                for cp in w_copies(nxt):
                    cp.start()

        if n_side:
            @pl.when(blk == 0)
            def _():
                for i in range(n_side):
                    side_in(i).start()

            @pl.when(blk == 2)
            def _():
                for i in range(n_side):
                    side_in(i).wait()
                for i in range(n_side):
                    side_out(i).start()

        def tile_body(t, _):
            rows = pl.ds(pl.multiple_of(t * TILE, TILE), TILE)
            if gather:
                for when, step in ((0, 0), (3, 1), (5, 2), (7, 3)):
                    pl.when(t == when)(steps[step])
            x = x_buf[rows, :]
            for j in range(4):
                z = jnp.dot(x, w_buf[blk, j, 0], preferred_element_type=F32)
                h_buf[:, j * DIM:(j + 1) * DIM] = gelu_kernel(z).astype(BF16)
            acc = jnp.dot(h_buf[...], jnp.concatenate([w_buf[blk, j, 1] for j in range(4)], 0), preferred_element_type=F32)
            x_buf[rows, :] = (x.astype(F32) + acc).astype(BF16)

            @pl.when(jnp.logical_and(blk == n_blk - 1, t > 0))
            def _():
                y_copy(t - 1).start()
                if to_out:
                    o_copy(t - 1).start()
            return 0
        lax.fori_loop(0, n_tiles, tile_body, 0)
        return 0

    lax.fori_loop(0, n_blk, blk_body, 0)
    y_copy(n_tiles - 1).start()
    if to_out:
        o_copy(n_tiles - 1).start()
    if gather:
        keep = [pltpu.make_async_copy(z_v, gathered[0], bounce[9].at[0]), pltpu.make_async_copy(m_v, gathered[1], bounce[9].at[1])]
        keep[0].start()
        steps[4]()
        keep[1].start()
        steps[5]()
        for cp in keep:
            cp.wait()
    for t in range(n_tiles):
        y_copy(t).wait()
        if to_out:
            o_copy(t).wait()
    for i in range(n_side):
        side_out(i).wait()


def run_forward(x, weights, chunk, name, to_out=False, out_buf=None, sides=(), piece=None):
    n_rows = chunk[-1]
    in_next = x.ndim > 2
    has_out_in = out_buf is not None
    side_rows = [(flip,) + where for _, flip, where in sides]
    sides = [rows for rows, _, _ in sides]
    spec = (in_next,) + chunk + (to_out, has_out_in)
    n_blk = len(weights)
    n_tiles = n_rows // TILE
    args = [x] + [w for pair in weights for w in pair] + ([piece] if piece is not None else []) + list(sides) + ([out_buf] if has_out_in else [])
    shapes, alias = [], {}
    if to_out:
        shapes.append(jax.ShapeDtypeStruct((16, ROWS, DIM), BF16))
        if has_out_in:
            alias = {len(args) - 1: 0}
    shapes.append(jax.ShapeDtypeStruct((n_rows, DIM), BF16))
    gather = piece is not None
    if gather:
        shapes += [jax.ShapeDtypeStruct((4, 2, HALF, DIM), BF16)] * 2
    scratch = [
        pltpu.VMEM((n_blk, 4, 2, DIM, DIM), BF16),
        pltpu.VMEM((n_rows, DIM), BF16),
        pltpu.VMEM((TILE, FFN), BF16),
        DMA((n_blk, 2)),
        DMA((2,)),
        ] + [DMA((n_tiles,))] * 2
    if gather:
        scratch += EXCHANGE_BUFS + EXCHANGE_SEMS + [DMA((2,))]
    if sides:
        scratch += [pltpu.VMEM((sum(k[-1] for k in side_rows), DIM), BF16), DMA((len(sides),)), DMA((len(sides),))]
    flops = n_rows * n_blk * 4 * DIM * FFN
    res = pl.pallas_call(
        functools.partial(forward_kernel, n_blk, spec, len(sides), tuple(side_rows), gather),
        out_shape=shapes, in_specs=[ANY] * len(args), out_specs=[ANY] * len(shapes),
        scratch_shapes=scratch, input_output_aliases=alias, name=name,
        cost_estimate=pl.CostEstimate(flops=flops, bytes_accessed=n_blk * 9 * MIB + n_rows * FFN, transcendentals=n_rows * n_blk * FFN),
        compiler_params=pltpu.CompilerParams(vmem_limit_bytes=VMEM_BIG, has_side_effects=gather),
    )(*args)
    return res if len(res) > 1 else res[0]


def copy_kernel(n_side, side_rows, *refs):
    side_refs, out_ref = refs[:n_side], refs[n_side + 1]
    side_buf, si_sem, so_sem = refs[n_side + 2:]
    stage = lax.axis_index('stage')
    starts = [sum(k[-1] for k in side_rows[:i]) for i in range(n_side)]

    def cp_in(i):
        return pltpu.make_async_copy(side_refs[i], side_buf.at[pl.ds(starts[i], side_rows[i][-1])], si_sem.at[i])

    def cp_out(i):
        flip, group, off, rows = side_rows[i]
        owner = stage if flip == OWN else jnp.bitwise_xor(stage, flip)
        return pltpu.make_async_copy(side_buf.at[pl.ds(starts[i], rows)], out_ref.at[4 * group + owner, pl.ds(off, rows)], so_sem.at[i])

    for i in range(n_side):
        cp_in(i).start()
    for i in range(n_side):
        cp_in(i).wait()
        cp_out(i).start()
    for i in range(n_side):
        cp_out(i).wait()


def run_copy(out_buf, sides, name):
    side_rows = [(flip,) + where for _, flip, where in sides]
    sides = [rows for rows, _, _ in sides]
    n_side = len(sides)
    rows = sum(k[-1] for k in side_rows)
    return pl.pallas_call(
        functools.partial(copy_kernel, n_side, tuple(side_rows)),
        out_shape=jax.ShapeDtypeStruct(out_buf.shape, BF16), in_specs=[ANY] * (n_side + 1), out_specs=ANY,
        scratch_shapes=[pltpu.VMEM((rows, DIM), BF16), DMA((n_side,)), DMA((n_side,))],
        input_output_aliases={n_side: 0}, name=name,
        cost_estimate=pl.CostEstimate(flops=rows * DIM * 300, bytes_accessed=rows * FFN, transcendentals=0),
        compiler_params=pltpu.CompilerParams(vmem_limit_bytes=VMEM_BIG),
    )(*sides, out_buf)


def update_kernel(scal_ref, g_ref, w_ref, m_ref, v_ref, wo_ref, mo_ref, vo_ref):
    w_new, m_new, v_new = adamw_update(w_ref[0], m_ref[0], v_ref[0], g_ref[0], scal_ref[0], scal_ref[1])
    wo_ref[0] = w_new
    mo_ref[0] = m_new
    vo_ref[0] = v_new


def run_update(scal, grad, w, m, v, name):
    rows = 192
    _, n_row, n_col = w.shape
    per = n_row // rows
    if n_col == FFN:
        par = pl.BlockSpec((1, rows, DIM), lambda j, i: (0, i, j))
        grid, g_spec = (4, 4), pl.BlockSpec((1, rows, DIM), lambda j, i: (j, i, 0))
    else:
        par = pl.BlockSpec((1, rows, DIM), lambda j, i: (0, 4 * j + i, 0))
        grid, g_spec = (4, 4), pl.BlockSpec((1, rows, DIM), lambda j, i: (j, i, 0))
    return pl.pallas_call(
        update_kernel, grid=grid,
        in_specs=[pl.BlockSpec(memory_space=pltpu.SMEM), g_spec, par, par, par], out_specs=[par] * 3,
        out_shape=[jax.ShapeDtypeStruct(w.shape, F32)] * 3, name=name,
        cost_estimate=pl.CostEstimate(flops=20_000_000_000, bytes_accessed=7 * 9 * MIB, transcendentals=n_row * n_col),
    )(scal, grad, w, m, v)


def ids():
    stage, rep = lax.axis_index('stage'), lax.axis_index('data')
    core = lax.rem(stage, 2)
    mate = stage + 1 - 2 * core
    return stage, core, rep, mate, [jnp.bitwise_xor(rep, k) for k in range(4)]


def push(src, dst, send_sem, recv_sem, data, stage):
    return pltpu.make_async_remote_copy(src_ref=src, dst_ref=dst, send_sem=send_sem, recv_sem=recv_sem, device_id=(data, stage), device_id_type=MESH_ID)


def exchange_steps(own, z_v, m_v, sems, before=None):
    ys, yr, zs, zr, ms, mr, ls = sems
    stage, _, rep, mate, near = ids()
    y_id, z_id, d_id = near[1:]

    def over_y(src, quarter, part, i):
        return push(src, z_v.at[quarter, part], ys.at[i], yr.at[i], y_id, stage)

    def over_z(src, quarter, part, i):
        return push(src, z_v.at[quarter, part], zs.at[i], zr.at[i], z_id, stage)

    def cross(quarter, part, src=None):
        i = quarter * 2 + part
        src = z_v.at[quarter, part] if src is None else src
        return push(src, m_v.at[quarter, part], ms.at[i], mr.at[i], rep, mate)

    def local(part):
        return pltpu.make_async_copy(own(part), z_v.at[rep, part], ls.at[part])

    def start():
        for part in (FIRST, SECOND):
            if before is not None:
                before(part)
            over_y(own(part), rep, part, part).start()
            over_z(own(part), rep, part, part).start()
            local(part).start()
            cross(rep, part, own(part)).start()

    def first():
        over_y(own(FIRST), y_id, FIRST, FIRST).wait_recv()
        over_z(z_v.at[y_id, FIRST], y_id, FIRST, SUMS).start()
        cross(y_id, FIRST).start()
        over_z(own(FIRST), z_id, FIRST, FIRST).wait_recv()
        cross(z_id, FIRST).start()

    def second():
        over_z(own(SECOND), z_id, SECOND, SECOND).wait_recv()
        over_y(z_v.at[z_id, SECOND], z_id, SECOND, SUMS).start()
        cross(z_id, SECOND).start()
        over_y(own(SECOND), y_id, SECOND, SECOND).wait_recv()
        cross(y_id, SECOND).start()

    def third():
        over_z(own(FIRST), d_id, FIRST, SUMS).wait_recv()
        cross(d_id, FIRST).start()
        over_y(own(SECOND), d_id, SECOND, SUMS).wait_recv()
        cross(d_id, SECOND).start()
        for part in (FIRST, SECOND):
            local(part).wait()

    def last():
        for quarter in range(4):
            for part in (FIRST, SECOND):
                cross(quarter, part).wait_recv()

    def drain():
        for i in range(3):
            over_y(own(FIRST), rep, FIRST, i).wait_send()
            over_z(own(FIRST), rep, FIRST, i).wait_send()
        for quarter in range(4):
            for part in (FIRST, SECOND):
                cross(quarter, part).wait_send()

    return start, first, second, third, last, drain


EXCHANGE_SEMS = [DMA((3,))] * 4 + [DMA((8,))] * 2 + [DMA((2,))]
EXCHANGE_BUFS = [pltpu.VMEM((4, 2, HALF, DIM), BF16)] * 2


def reduce_kernel(h_ref, g_ref, a_ref, p_ref, acc2_ref, acc1_ref, r2_ref, r1_ref,
                  g_v, a_v, b_v, part, ry, rz, in_sem, b_sem, acc_sem, ys, yr, zs, zr, o_sem):
    stage, _, rep, _, near = ids()
    y_id, z_id = near[1], near[2]
    top, low = pl.ds(0, HALF), pl.ds(HALF, HALF)
    fixed = [pltpu.make_async_copy(g_ref, g_v, in_sem.at[0]), pltpu.make_async_copy(a_ref.at[0], a_v, in_sem.at[1])]

    def target(i):
        return jnp.bitwise_xor(rep, jnp.where(i == DIAG, SELF, jnp.where(i == SELF, DIAG, i)))

    def cols(i):
        return pl.ds(pl.multiple_of(target(i) * DIM, DIM), DIM)

    def loads(mat, i):
        slot = lax.rem(i, 2)
        if mat == 0:
            block, acc = h_ref.at[:, cols(i)], acc2_ref.at[0, 0, cols(i), :]
        else:
            block, acc = p_ref.at[:, cols(i)], acc1_ref.at[0, 0, :, cols(i)]
        return [pltpu.make_async_copy(block, b_v.at[slot], b_sem.at[mat, i]), pltpu.make_async_copy(acc, part.at[mat, i], acc_sem.at[mat, i])]

    def over_y(mat, i, rows, k):
        return push(part.at[mat, i, rows, :], ry.at[mat, k], ys.at[mat, k], yr.at[mat, k], y_id, stage)

    def over_z(mat, i, rows, k):
        return push(part.at[mat, i, rows, :], rz.at[mat, k], zs.at[mat, k], zr.at[mat, k], z_id, stage)

    for cp in loads(0, 0) + fixed:
        cp.start()
    for mat in range(2):
        fixed[mat].wait()

        def body(i, _):
            @pl.when(i < SELF)
            def _():
                for cp in loads(mat, i + 1):
                    cp.start()
            if mat == 0:
                @pl.when(i == SELF)
                def _():
                    for cp in loads(1, 0):
                        cp.start()
            for cp in loads(mat, i):
                cp.wait()
            block = b_v[lax.rem(i, 2)]
            lhs, rhs = (block, g_v[...]) if mat == 0 else (a_v[...], block)
            part[mat, i] = part[mat, i] + lax.dot_general(lhs, rhs, FIRST_DIMS, preferred_element_type=F32)

            @pl.when(i == DIAG)
            def _():
                over_y(mat, i, top, LONG).start()
                over_z(mat, i, low, LONG).start()

            @pl.when(i == SIDE_Y)
            def _():
                over_y(mat, i, top, SHORT).start()

            @pl.when(i == SIDE_Z)
            def _():
                over_z(mat, i, low, SHORT).start()
            return 0
        lax.fori_loop(0, 4, body, 0)

    def add(mat, i, base, buf, k):
        def body(t, _):
            rows = pl.ds(pl.multiple_of(t * STRIP, STRIP), STRIP)
            here = pl.ds(pl.multiple_of(base + t * STRIP, STRIP), STRIP)
            part[mat, i, here, :] = part[mat, i, here, :] + buf[mat, k, rows, :]
            return 0
        lax.fori_loop(0, HALF // STRIP, body, 0)

    for mat in range(2):
        over_y(mat, DIAG, top, LONG).wait_recv()
        add(mat, SIDE_Z, 0, ry, LONG)
        over_z(mat, SIDE_Z, top, SUMS).start()
        over_z(mat, DIAG, low, LONG).wait_recv()
        add(mat, SIDE_Y, HALF, rz, LONG)
        over_y(mat, SIDE_Y, low, SUMS).start()
    for mat in range(2):
        over_y(mat, SIDE_Y, top, SHORT).wait_recv()
        add(mat, SELF, 0, ry, SHORT)
        over_z(mat, SIDE_Z, low, SHORT).wait_recv()
        add(mat, SELF, HALF, rz, SHORT)
    outs = [pltpu.make_async_copy(part.at[mat, SELF], ref.at[0], o_sem.at[mat]) for mat, ref in ((0, r2_ref), (1, r1_ref))]
    for mat in range(2):
        over_z(mat, SIDE_Z, top, SUMS).wait_recv()
        add(mat, SELF, 0, rz, SUMS)
        over_y(mat, SIDE_Y, low, SUMS).wait_recv()
        add(mat, SELF, HALF, ry, SUMS)
        outs[mat].start()
    for mat in range(2):
        for k in (LONG, SHORT, SUMS):
            over_y(mat, DIAG, top, k).wait_send()
            over_z(mat, DIAG, top, k).wait_send()
        outs[mat].wait()


def run_reduce(act_h, grad, acts, d_pre, acc_second, acc_first):
    shard = jax.ShapeDtypeStruct((1, DIM, DIM), F32)
    return pl.pallas_call(
        reduce_kernel, in_specs=[ANY] * 6, out_specs=[ANY] * 2, out_shape=[shard, shard], name='reduce',
        scratch_shapes=[pltpu.VMEM((ROWS, DIM), BF16), pltpu.VMEM((ROWS, DIM), BF16), pltpu.VMEM((2, ROWS, DIM), BF16),
                        pltpu.VMEM((2, 4, DIM, DIM), F32), pltpu.VMEM((2, 3, HALF, DIM), F32), pltpu.VMEM((2, 3, HALF, DIM), F32),
                        DMA((2,)), DMA((2, 4)), DMA((2, 4))] + [DMA((2, 3))] * 4 + [DMA((2,))],
        cost_estimate=pl.CostEstimate(flops=150_000_000_000, bytes_accessed=70 * MIB, transcendentals=0),
        compiler_params=pltpu.CompilerParams(vmem_limit_bytes=VMEM_BIG, has_side_effects=True),
    )(act_h, grad, acts, d_pre, acc_second, acc_first)


def gelu_grad(z):
    z_sq = z * z
    t = jnp.tanh(z * (ROOT + ROOT * CUBE * z_sq))
    return 0.5 + 0.5 * t + (0.5 * z) * (1.0 - t * t) * (ROOT + 3.0 * ROOT * CUBE * z_sq)


N_CHUNK = 8


def backward_kernel(a_ref, d_ref, w1_ref, w2_ref, h_ref, dz_ref, g_ref, a_v, w1_v, w2_v, z_v, g_v, h_b, p_b, s_b,
                    in_sem, h_sem, p_sem, o_sem, send_sem, recv_sem):
    stage = lax.axis_index('stage')
    rep = lax.axis_index('data')
    rows = a_v.shape[0] // N_CHUNK
    below = jnp.maximum(stage - 1, 0)
    cp_a = pltpu.make_async_copy(a_ref.at[0], a_v, in_sem.at[0])
    cp_1 = pltpu.make_async_copy(w1_ref, w1_v, in_sem.at[1])
    cp_2 = pltpu.make_async_copy(w2_ref, w2_v, in_sem.at[2])
    cp_a.start()
    cp_1.start()
    cp_2.start()
    n_pre = jnp.where(stage == 3, 0, jnp.where(stage == 2, 4, N_CHUNK))

    def d_copy(k):
        return pltpu.make_async_copy(d_ref.at[pl.ds(pl.multiple_of(k * rows, rows), rows)], g_v.at[k], recv_sem.at[k])

    @pl.when(stage == 3)
    def _():
        def body(k, _):
            d_copy(k).start()
            return 0
        lax.fori_loop(0, N_CHUNK, body, 0)

    def out_copy(buf, ref, sem, k):
        return pltpu.make_async_copy(buf, ref.at[pl.ds(pl.multiple_of(k * rows, rows), rows)], sem.at[k])

    def h_copy(k):
        return out_copy(h_b.at[lax.rem(k, 2)], h_ref, h_sem, k)

    def p_copy(k):
        return out_copy(p_b.at[lax.rem(k, 2)], dz_ref, p_sem, k)

    def g_copy(k):
        return out_copy(g_v.at[k], g_ref, o_sem, k)

    def send(k):
        return push(s_b.at[k], g_v.at[k], send_sem.at[k], recv_sem.at[k], rep, below)

    def z_body(k, _):
        @pl.when(k >= 2)
        def _():
            h_copy(k - 2).wait()
        a = a_v[pl.ds(pl.multiple_of(k * rows, rows), rows), :]
        slot = lax.rem(k, 2)
        for j in range(4):
            cols = slice(j * DIM, (j + 1) * DIM)
            z = jnp.dot(a, w1_v[:, cols], preferred_element_type=F32)
            z_v[k, :, cols] = z
            h_b[slot, :, cols] = gelu_kernel(z).astype(BF16)
        h_copy(k).start()
        return 0

    cp_a.wait()
    cp_1.wait()
    lax.fori_loop(0, n_pre, z_body, 0)
    cp_2.wait()

    def chain_body(k, _):
        lax.fori_loop(k, jnp.where(k >= n_pre, k + 1, k), z_body, 0)
        d_copy(k).wait()

        @pl.when(k >= 2)
        def _():
            p_copy(k - 2).wait()
        g_copy(k).start()
        g = g_v[k]
        slot = lax.rem(k, 2)
        acc = None
        for j in range(4):
            cols = slice(j * DIM, (j + 1) * DIM)
            d_hid = lax.dot_general(g, w2_v[cols, :], TRANS_DIMS, preferred_element_type=F32)
            d_pre = (gelu_grad(z_v[k, :, cols]) * d_hid).astype(BF16)
            p_b[slot, :, cols] = d_pre
            part = lax.dot_general(d_pre, w1_v[:, cols], TRANS_DIMS, preferred_element_type=F32)
            acc = part if acc is None else acc + part
        s_b[k] = (g.astype(F32) + acc).astype(BF16)

        @pl.when(stage > 0)
        def _():
            send(k).start()
        p_copy(k).start()
        return 0

    lax.fori_loop(0, N_CHUNK, chain_body, 0)

    @pl.when(stage > 0)
    def _():
        def body(k, _):
            send(k).wait_send()
            return 0
        lax.fori_loop(0, N_CHUNK, body, 0)
    for k in (N_CHUNK - 2, N_CHUNK - 1):
        h_copy(k).wait()
        p_copy(k).wait()

    def fin(k, _):
        g_copy(k).wait()
        return 0
    lax.fori_loop(0, N_CHUNK, fin, 0)


def run_backward(acts, d_out, w1, w2):
    n = d_out.shape[0]
    rows = n // N_CHUNK
    return pl.pallas_call(
        backward_kernel, in_specs=[ANY] * 4, out_specs=[ANY] * 3, name='backward',
        out_shape=[jax.ShapeDtypeStruct((n, FFN), BF16), jax.ShapeDtypeStruct((n, FFN), BF16), jax.ShapeDtypeStruct((n, DIM), BF16)],
        scratch_shapes=[
            pltpu.VMEM((n, DIM), BF16), pltpu.VMEM((DIM, FFN), BF16), pltpu.VMEM((FFN, DIM), BF16),
            pltpu.VMEM((N_CHUNK, rows, FFN), F32), pltpu.VMEM((N_CHUNK, rows, DIM), BF16),
            pltpu.VMEM((2, rows, FFN), BF16), pltpu.VMEM((2, rows, FFN), BF16), pltpu.VMEM((N_CHUNK, rows, DIM), BF16),
            DMA((3,)), DMA((N_CHUNK,)), DMA((N_CHUNK,)),
            DMA((N_CHUNK,)), DMA((N_CHUNK,)), DMA((N_CHUNK,))],
        cost_estimate=pl.CostEstimate(flops=6 * n * DIM * FFN, bytes_accessed=50_000_000, transcendentals=2 * n * FFN),
        compiler_params=pltpu.CompilerParams(vmem_limit_bytes=VMEM_BIG, has_side_effects=True),
    )(acts, d_out, w1, w2)


def middle_kernel(lr_ref, mx_ref, r1_ref, r2_ref, w1_ref, m1_ref, v1_ref, w2_ref, m2_ref, v2_ref,
                  own_ref, mate_ref, q1_ref, q2_ref, q3_ref, scal_ref,
                  p_v, q_v, z_v, m_v, s_v, n_v, in_sem, ns, nr, hs, hr, xs, xr, o_sem, *sems):
    stage = lax.axis_index('stage')
    rep = lax.axis_index('data')
    core = lax.rem(stage, 2)
    side = lax.div(stage, 2)
    base = 2 * side
    me = rep * 4 + stage

    cols = pl.ds(pl.multiple_of(rep * DIM, DIM), DIM)
    srcs = [r1_ref.at[0], r2_ref.at[0], w1_ref.at[0, :, cols], m1_ref.at[0, :, cols], v1_ref.at[0, :, cols],
            w2_ref.at[0, cols, :], m2_ref.at[0, cols, :], v2_ref.at[0, cols, :]]
    loads = [pltpu.make_async_copy(srcs[i], p_v.at[i], in_sem.at[i]) for i in range(8)]
    for cp in loads:
        cp.start()
    loads[0].wait()
    loads[1].wait()

    def sq_body(t, acc):
        rows = pl.ds(pl.multiple_of(t * 64, 64), 64)
        a = p_v[0, rows, :]
        b = p_v[1, rows, :]
        return acc + a * a + b * b
    acc = lax.fori_loop(0, 12, sq_body, jnp.zeros((64, DIM), F32))
    n_v[me] = jnp.full((8, 128), jnp.sum(acc), F32)

    def norm_send(i, peer):
        return push(n_v.at[me], n_v.at[me], ns.at[i], nr.at[i], lax.div(peer, 4), lax.rem(peer, 4))

    def peer_of(i):
        return lax.rem(me + i, 16)

    for i in range(1, 16):
        norm_send(i, peer_of(i)).start()
    for i in range(1, 16):
        norm_send(i, peer_of(i)).wait()
    total = n_v[0]
    for i in range(1, 16):
        total = total + n_v[i]
    norm = jnp.sqrt(total[0:1, 0:1] * 0.0625)
    clip = jnp.minimum(1.0, mx_ref[0] / (norm + NORM_EPS)) * 0.25
    scal_ref[...] = jnp.broadcast_to(clip, (8, 128))
    for cp in loads[2:]:
        cp.wait()
    lr = lr_ref[0]

    def upd(half, dst):
        for k in range(2):
            def body(t, _):
                rows = pl.ds(pl.multiple_of(half * HALF + t * 64, 64), 64)
                new = adamw_update(p_v[2 + 3 * k, rows, :], p_v[3 + 3 * k, rows, :], p_v[4 + 3 * k, rows, :], p_v[k, rows, :], clip, lr)[0]
                dst[k, pl.ds(pl.multiple_of(t * 64, 64), 64), :] = new.astype(BF16)
                return 0
            lax.fori_loop(0, 6, body, 0)

    mate = base + 1 - core
    far = lax.rem(stage + 2, 4)
    upd(1 - core, s_v)
    half_cp = push(s_v, q_v.at[stage], hs, hr, rep, mate)
    half_cp.start()
    upd(core, q_v.at[stage])
    half_cp.wait_send()
    push(s_v, q_v.at[mate], hs, hr, rep, mate).wait_recv()

    def x_part(blk, i):
        src = q_v.at[blk + i // 2, i % 2]
        return push(src, src, xs.at[i], xr.at[i], rep, far)

    x_out = [x_part(base, i) for i in range(4)]
    x_in = [x_part(2 - base, i) for i in range(4)]
    for cp in x_out:
        cp.start()

    def before(part):
        @pl.when(side == 1)
        def _():
            x_in[part].wait_recv()

    steps = exchange_steps(lambda part: q_v.at[0, part], z_v, m_v, sems, before)
    for step in steps[:4]:
        step()
    outs = [pltpu.make_async_copy(z_v, own_ref, o_sem.at[0])]

    @pl.when(side == 0)
    def _():
        x_in[0].wait_recv()
        x_in[1].wait_recv()
    x_in[2].wait_recv()
    x_in[3].wait_recv()
    outs += [pltpu.make_async_copy(q_v.at[b], r, o_sem.at[b]) for b, r in enumerate((q1_ref, q2_ref, q3_ref), 1)]
    for cp in outs:
        cp.start()
    steps[4]()
    outs.append(pltpu.make_async_copy(m_v, mate_ref, o_sem.at[4]))
    outs[4].start()
    for cp in x_out:
        cp.wait_send()
    steps[5]()
    for cp in outs:
        cp.wait()


def run_middle(lr, mx, r1, r2, w1, m1, v1, w2, m2, v2):
    smem = pl.BlockSpec(memory_space=pltpu.SMEM)
    piece = jax.ShapeDtypeStruct((2, HALF, DIM), BF16)
    block = jax.ShapeDtypeStruct((4, 2, HALF, DIM), BF16)
    return pl.pallas_call(
        middle_kernel, in_specs=[smem, smem] + [ANY] * 8,
        out_specs=[ANY] * 5 + [pl.BlockSpec(memory_space=pltpu.VMEM)],
        out_shape=[block, block, piece, piece, piece, jax.ShapeDtypeStruct((8, 128), F32)], name='middle',
        scratch_shapes=[
            pltpu.VMEM((8, DIM, DIM), F32), pltpu.VMEM((4, 2, HALF, DIM), BF16)] + EXCHANGE_BUFS + [
            pltpu.VMEM((2, HALF, DIM), BF16), pltpu.VMEM((16, 8, 128), F32), DMA((8,)), DMA((16,)), DMA((16,)), DMA, DMA, DMA((4,)), DMA((4,)), DMA((5,))] + EXCHANGE_SEMS,
        cost_estimate=pl.CostEstimate(flops=60_000_000_000, bytes_accessed=40_000_000, transcendentals=0),
        compiler_params=pltpu.CompilerParams(vmem_limit_bytes=VMEM_BIG, has_side_effects=True),
    )(lr, mx, r1, r2, w1, m1, v1, w2, m2, v2)


def solution(mesh):
    w_spec = P('stage', None, None)
    acc_spec = P('data', 'stage', None, None)
    row_spec = P(None, 'data', None)

    def stage_program(w_in, w_out, mom_in, mom_out, var_in, var_out, acc_in, acc_out, stage_acts, d_out, next_x, learn_rate, max_norm):
        w_first = w_in[0].astype(BF16)
        w_second = w_out[0].astype(BF16)
        act_h, pre_keep, grad_keep = run_backward(stage_acts, d_out, w_first, w_second)
        sh_second, sh_first = run_reduce(act_h, grad_keep, stage_acts, pre_keep, acc_out, acc_in)
        own, mate, piece1, piece2, piece3, scal = run_middle(learn_rate, max_norm, sh_first, sh_second, w_in, mom_in, var_in, w_out, mom_out, var_out)
        scal = jnp.stack([scal[0, 0], learn_rate[0]])
        weights = [(own, mate)]
        rows_a = next_x
        both = CHUNK_0[:-1] + (2 * ROWS,)
        for blk, piece in enumerate((piece1, piece2, piece3)):
            rows_a, own, mate = run_forward(rows_a, weights[blk:], both, f'fwd_a{blk}', piece=piece)
            weights.append((own, mate))
        sh_second, sh_first, rows_a = lax.optimization_barrier((sh_second, sh_first, rows_a))
        y_0 = run_forward(rows_a, weights[-1:], CHUNK_0, 'fwd_a3')
        rows_a, y_0 = lax.optimization_barrier((rows_a, y_0))
        y_1 = run_forward(rows_a, weights[-1:], CHUNK_0[:1] + (ROWS, ROWS), 'fwd_a4')

        def to_mate(rows):
            return lax.ppermute(rows, 'stage', CORE_PERM)

        def to_far(rows):
            return lax.ppermute(rows, 'stage', X_PERM)

        far_0, far_1, mate_0, mate_1 = to_far(y_0), to_far(y_1), to_mate(y_0), to_mate(y_1)
        out, y_2 = run_forward(next_x, weights, CHUNK_2, 'fwd_b', to_out=True)
        far_0, mate_0, mate_1, y_2 = lax.optimization_barrier((far_0, mate_0, mate_1, y_2))
        relay_0 = to_mate(far_0)
        far_2, mate_2 = to_far(y_2), to_mate(y_2)
        sides = [(y_0, OWN, CHUNK_0), (y_1, OWN, CHUNK_1), (mate_0, MATE, CHUNK_0), (mate_1, MATE, CHUNK_1)]
        out, y_3 = run_forward(next_x, weights, CHUNK_3, 'fwd_c', to_out=True, out_buf=out, sides=sides)
        far_1, y_3 = lax.optimization_barrier((far_1, y_3))
        relay_1 = to_mate(far_1)
        far_3, mate_3 = to_far(y_3), to_mate(y_3)
        sides = [(far_0, FAR, CHUNK_0), (relay_0, RELAY, CHUNK_0), (mate_2, MATE, CHUNK_2)]
        out, y_4 = run_forward(next_x, weights, CHUNK_4, 'fwd_d', to_out=True, out_buf=out, sides=sides)
        full_second = lax.all_gather(sh_second[0], 'data')
        full_first = lax.all_gather(sh_first[0], 'data')
        scal, y_4 = lax.optimization_barrier((scal, y_4))
        far_4, mate_4 = to_far(y_4), to_mate(y_4)
        new_second, mom_second, sec_second = run_update(scal, full_second, w_out, mom_out, var_out, 'upd_second')
        far_2, new_second, scal = lax.optimization_barrier((far_2, new_second, scal))
        relay_2 = to_mate(far_2)
        new_first, mom_first, sec_first = run_update(scal, full_first, w_in, mom_in, var_in, 'upd_first')
        far_3, new_first = lax.optimization_barrier((far_3, new_first))
        relay_3, relay_4 = to_mate(far_3), to_mate(far_4)
        out = run_copy(out, [(far_1, FAR, CHUNK_1), (relay_1, RELAY, CHUNK_1), (mate_3, MATE, CHUNK_3), (far_2, FAR, CHUNK_2)], 'put_a')
        out = run_copy(out, [(relay_2, RELAY, CHUNK_2), (far_3, FAR, CHUNK_3), (relay_3, RELAY, CHUNK_3), (mate_4, MATE, CHUNK_4), (far_4, FAR, CHUNK_4), (relay_4, RELAY, CHUNK_4)], 'put_b')
        return (new_first, new_second, mom_first, mom_second, sec_first, sec_second, out)

    return jax.shard_map(stage_program, mesh=mesh, in_specs=(w_spec, w_spec, w_spec, w_spec, w_spec, w_spec, acc_spec, acc_spec, P('stage', 'data', None), P('data', None), row_spec, P(None), P(None)), out_specs=(w_spec, w_spec, w_spec, w_spec, w_spec, w_spec, row_spec), check_vma=False)
```

time: 2970 us -> 853 us (0.29)
  waiting for transfers between devices: 1400 us -> 0.08 us
  Pallas kernels: 0 us -> 809 us
  starting transfers between devices: 598 us -> 8.24 us
  matrix products: 523 us -> 0 us
  local copies, waits for them, and re-layouts: 227 us -> 2.55 us
  other arithmetic: 188 us -> 10.9 us
    psum x2 -> x0, waiting for transfers between devices: 1180 us -> none  [the longest x1 870 us: stage_program(): lax.psum(jnp.where(stage_idx == last_stage, out_buf, jnp.zeros_like(out_b...]
    pallas_call x0 -> x15, Pallas kernels: none -> 809 us  [the longest x8 422 us: run_forward(): pl.pallas_call(functools.partial(forward_kernel, n_blk, spec, len(sides),...]
    ppermute x21 -> x15, starting transfers between devices: 598 us -> 7.95 us  [the longest x5 5.72 us: to_far(): return lax.ppermute(rows, 'stage', X_PERM)]
    dot_general x20 -> x0, matrix products: 523 us -> none  [the longest x16 404 us: block_forward(): branch = jnp.dot(act_h, w_second, preferred_element_type=jnp.float32)]
    ppermute x21 -> x15, waiting for transfers between devices: 220 us -> 0.04 us  [the longest x10 0.03 us: to_mate(): return lax.ppermute(rows, 'stage', CORE_PERM)]
    unnamed x15 -> x2, local copies, waits for them, and re-layouts: 105 us -> 1.37 us
    convert_element_type x4 -> x2, other arithmetic: 69.7 us -> 9.58 us  [the longest x1 6.69 us: stage_program(): w_second = w_out[0].astype(BF16)]
    select_n x20 -> x0, other arithmetic: 58.4 us -> none  [the longest x19 42.1 us: fwd_step(): row_block = jnp.where(stage_idx == 0, first_in, recv_buf)]
  transfers between devices with their start and end apart: 23 -> 17, of which waited for: 5 -> 0; matrix products, arithmetic and copies ran while one was open for 4% -> 0% of each run, Pallas kernels for 0% -> 36%
where the time goes in v1:
time: 853 us; the launch traced here: 846 us
  Pallas kernels  809 us (95%)
  between operations  16 us (2%)
  other arithmetic  10.9 us (1%)
    pallas_call x8, Pallas kernels, run_forward(): pl.pallas_call(functools.partial(forward_kernel, n_blk, spec, len(sides),...  422 us
    pallas_call x1, Pallas kernels, run_reduce(): pl.pallas_call(reduce_kernel, in_specs=[ANY] * 6, out_specs=[ANY] * 2, ou...  167 us
    pallas_call x1, Pallas kernels, run_middle(): pl.pallas_call(middle_kernel, in_specs=[smem, smem] + [ANY] * 8, out_spec...  74 us
    pallas_call x1, Pallas kernels, run_backward(): pl.pallas_call(backward_kernel, in_specs=[ANY] * 4, out_specs=[ANY] * 3,...  73.5 us
    pallas_call x2, Pallas kernels, run_update(): pl.pallas_call(update_kernel, grid=grid, in_specs=[pl.BlockSpec(memory_sp...  55.2 us
    pallas_call x2, Pallas kernels, run_copy(): pl.pallas_call(functools.partial(copy_kernel, n_side, tuple(side_rows)),...  17.2 us
  transfers between devices with their start and end apart: 17, of which 0 were waited for; matrix products, arithmetic and copies ran while one was open for 0% of the time, Pallas kernels for 36%

profile of v1, /device:TPU:0, one launch (start us, length us, event | category | flops | bytes accessed | tf_op | source)
XLA Modules:
  0.0 846.4 jit_solution(751444582165886612)
XLA Ops:
  7.2 6.7 convert_bitcast_fusion.w2_ref
  13.9 1.4 copy-done
  15.3 2.9 convert_bitcast_fusion.1.w1_ref
  19.5 73.5 %backward.1 = (bf16[2048,3072]{1,0:T(8,128)(2,1)}, bf16[2048,3072]{1,0:T(8,128)(2,1)}, bf16[2048,768]{1,0:T(8,128)(2,1)}) custom-call(bf16[1,2048,768]{2,1,0:T(8,128)(2,1)} %a_ref.3, bf16[2048,768]{1,0:T(8,128)(2,1)} %d_ref.1, bf16[768,3072]{1,0:T(8,128)(2,1)} %convert_bitcast_fusion.1.w1_ref, bf16[3072,768]{1,0:T(8,128)(2,1)} %convert_bitcast_fusion.w2_ref), custom_call_target="tpu_custom_call" | custom-call | flops 28991029248 | bytes 50000000 | tf_op jit(solution)/shard_map/backward/pallas_call | solution.py:601
  93.0 166.8 %reduce.1 = (f32[1,768,768]{2,1,0:T(8,128)}, f32[1,768,768]{2,1,0:T(8,128)}) custom-call(bf16[2048,3072]{1,0:T(8,128)(2,1)} %get-tuple-element.57.h_ref, bf16[2048,768]{1,0:T(8,128)(2,1)} %get-tuple-element.58.g_ref, bf16[1,2048,768]{2,1,0:T(8,128)(2,1)} %a_ref.3, bf16[2048,3072]{1,0:T(8,128)(2,1)} %get-tuple-element.59.p_ref, f32[1,1,3072,768]{3,2,1,0:T(8,128)} %acc2_ref.1, ...), custom_call_target="tpu_custom_call" | custom-call | flops 149999992832 | bytes 73400320 | tf_op jit(solution)/shard_map/reduce/pallas_call | solution.py:477
  259.9 74.0 %middle.1 = (bf16[4,2,384,768]{3,2,1,0:T(8,128)(2,1)}, bf16[4,2,384,768]{3,2,1,0:T(8,128)(2,1)}, bf16[2,384,768]{2,1,0:T(8,128)(2,1)}, bf16[2,384,768]{2,1,0:T(8...) custom-call(f32[1]{0:T(128)S(6)} %copy.28.lr_ref, f32[1]{0:T(128)S(6)} %copy.29.mx_ref, ...), custom_call_target="tpu_custom_call" | custom-call | flops 60000002048 | bytes 40000000 | tf_op jit(solution)/shard_map/middle/pallas_call | solution.py:722
  333.9 61.8 %fwd_a0.1 = (bf16[4096,768]{1,0:T(8,128)(2,1)}, bf16[4,2,384,768]{3,2,1,0:T(8,128)(2,1)}, bf16[4,2,384,768]{3,2,1,0:T(8,128)(2,1)}) custom-call(bf16[16,2048,768]{2,1,0:T(8,128)(2,1)} %refs_0_.7, bf16[4,2,384,768]{3,2,1,0:T(8,128)(2,1)} %get-tuple-element.62.refs_1_, bf16[4,2,384,768]{3,2,1,0:T(8,128)(2,1)} %get-tuple-element.63.refs_2_, ...), custom_call_target="tpu_custom_call" | custom-call | flops 38654705664 | bytes 22020096 | tf_op jit(solution)/shard_map/fwd_a0/pallas_call | solution.py:224
  395.7 58.6 %fwd_a1.1 = (bf16[4096,768]{1,0:T(8,128)(2,1)}, bf16[4,2,384,768]{3,2,1,0:T(8,128)(2,1)}, bf16[4,2,384,768]{3,2,1,0:T(8,128)(2,1)}) custom-call(bf16[4096,768]{1,0:T(8,128)(2,1)} %get-tuple-element.65.refs_0_, bf16[4,2,384,768]{3,2,1,0:T(8,128)(2,1)} %get-tuple-element.66.refs_1_.refs_3_, bf16[4,2,384,768]{3,2,1,0:T(8,128)(2,1)} %get-tuple-element.67.refs_2_.refs_4_, ...), custom_call_target="tpu_custom_call" | custom-call | flops 38654705664 | bytes 22020096 | tf_op jit(solution)/shard_map/fwd_a1/pallas_call | solution.py:224
  454.3 58.6 %fwd_a2.1 = (bf16[4096,768]{1,0:T(8,128)(2,1)}, bf16[4,2,384,768]{3,2,1,0:T(8,128)(2,1)}, bf16[4,2,384,768]{3,2,1,0:T(8,128)(2,1)}) custom-call(bf16[4096,768]{1,0:T(8,128)(2,1)} %get-tuple-element.69.refs_0_, bf16[4,2,384,768]{3,2,1,0:T(8,128)(2,1)} %get-tuple-element.70.refs_1_.refs_5_, bf16[4,2,384,768]{3,2,1,0:T(8,128)(2,1)} %get-tuple-element.71.refs_2_.refs_6_, ...), custom_call_target="tpu_custom_call" | custom-call | flops 38654705664 | bytes 22020096 | tf_op jit(solution)/shard_map/fwd_a2/pallas_call | solution.py:224
  513.2 27.1 %fwd_a3.1.refs_9_ = bf16[2048,768]{1,0:T(8,128)(2,1)} custom-call(bf16[4096,768]{1,0:T(8,128)(2,1)} %get-tuple-element.77.refs_0_, bf16[4,2,384,768]{3,2,1,0:T(8,128)(2,1)} %get-tuple-element.75.refs_1_.refs_7_, bf16[4,2,384,768]{3,2,1,0:T(8,128)(2,1)} %get-tuple-element.76.refs_2_.refs_8_), custom_call_target="tpu_custom_call" | custom-call | flops 19327352832 | bytes 15728640 | tf_op jit(solution)/shard_map/fwd_a3/pallas_call | solution.py:224
  540.3 1.5 collective-permute-start.1
  541.8 27.1 %fwd_a4.1.refs_10_ = bf16[2048,768]{1,0:T(8,128)(2,1)} custom-call(bf16[4096,768]{1,0:T(8,128)(2,1)} %get-tuple-element.77.refs_0_, bf16[4,2,384,768]{3,2,1,0:T(8,128)(2,1)} %get-tuple-element.75.refs_1_.refs_7_, bf16[4,2,384,768]{3,2,1,0:T(8,128)(2,1)} %get-tuple-element.76.refs_2_.refs_8_), custom_call_target="tpu_custom_call" | custom-call | flops 19327352832 | bytes 15728640 | tf_op jit(solution)/shard_map/fwd_a4/pallas_call | solution.py:224
  569.5 0.6 collective-permute-start
  570.1 91.5 %fwd_b.1 = (bf16[16,2048,768]{2,1,0:T(8,128)(2,1)}, bf16[2048,768]{1,0:T(8,128)(2,1)}) custom-call(bf16[16,2048,768]{2,1,0:T(8,128)(2,1)} %refs_0_.7, bf16[4,2,384,768]{3,2,1,0:T(8,128)(2,1)} %get-tuple-element.62.refs_1_, bf16[4,2,384,768]{3,2,1,0:T(8,128)(2,1)} %get-tuple-element.63.refs_2_, bf16[4,2,384,768]{3,2,1,0:T(8,128)(2,1)} %get-tuple-element.66.refs_1_.refs_3_, ...), custom_call_target="tpu_custom_call" | custom-call | flops 77309411328 | bytes 44040192 | tf_op jit(solution)/shard_map/fwd_b/pallas_call | solution.py:224
  661.6 1.2 slice.3
  662.7 1.3 pad_maximum_fusion.scal_ref
  664.1 1.6 collective-permute-start.5
  665.8 48.6 %fwd_c.1 = (bf16[16,2048,768]{2,1,0:T(8,128)(2,1)}, bf16[1024,768]{1,0:T(8,128)(2,1)}) custom-call(bf16[16,2048,768]{2,1,0:T(8,128)(2,1)} %refs_0_.7, bf16[4,2,384,768]{3,2,1,0:T(8,128)(2,1)} %get-tuple-element.62.refs_1_, bf16[4,2,384,768]{3,2,1,0:T(8,128)(2,1)} %get-tuple-element.63.refs_2_, ...), custom_call_target="tpu_custom_call", output_to_operand_aliasing={{0}: (13, {})} | custom-call | flops 38654705664 | bytes 40894464 | tf_op jit(solution)/shard_map/fwd_c/pallas_call | solution.py:224
  715.3 48.6 %fwd_d.1 = (bf16[16,2048,768]{2,1,0:T(8,128)(2,1)}, bf16[1024,768]{1,0:T(8,128)(2,1)}) custom-call(bf16[16,2048,768]{2,1,0:T(8,128)(2,1)} %refs_0_.7, bf16[4,2,384,768]{3,2,1,0:T(8,128)(2,1)} %get-tuple-element.62.refs_1_, bf16[4,2,384,768]{3,2,1,0:T(8,128)(2,1)} %get-tuple-element.63.refs_2_, ...), custom_call_target="tpu_custom_call", output_to_operand_aliasing={{0}: (12, {})} | custom-call | flops 38654705664 | bytes 40894464 | tf_op jit(solution)/shard_map/fwd_d/pallas_call | solution.py:224
  763.9 1.6 collective-permute-start.11
  765.5 27.6 %upd_second.1 = (f32[1,3072,768]{2,1,0:T(8,128)}, f32[1,3072,768]{2,1,0:T(8,128)}, f32[1,3072,768]{2,1,0:T(8,128)}) custom-call(f32[2]{0:T(128)} %pad_maximum_fusion.scal_ref, f32[4,768,768]{2,1,0:T(8,128)} %all-gather.3.cloned.1.call-done.g_ref, f32[1,3072,768]{2,1,0:T(8,128)} %w_ref.2, f32[1,3072,768]{2,1,0:T(8,128)} %m_ref.2, f32[1,3072,768]{2,1,0:T(8,128)} %v_ref.2), custom_call_target="tpu_custom_call" | custom-call | flops 20000000000 | bytes 66060288 | tf_op jit(solution)/shard_map/upd_second/pallas_call | solution.py:289
  793.3 27.6 %upd_first.1 = (f32[1,768,3072]{2,1,0:T(8,128)}, f32[1,768,3072]{2,1,0:T(8,128)}, f32[1,768,3072]{2,1,0:T(8,128)}) custom-call(f32[2]{0:T(128)} %pad_maximum_fusion.scal_ref, f32[4,768,768]{2,1,0:T(8,128)} %all-gather.5.cloned.1.call-done.g_ref, f32[1,768,3072]{2,1,0:T(8,128)} %w_ref.3, f32[1,768,3072]{2,1,0:T(8,128)} %m_ref.3, f32[1,768,3072]{2,1,0:T(8,128)} %v_ref.3), custom_call_target="tpu_custom_call" | custom-call | flops 20000000000 | bytes 66060288 | tf_op jit(solution)/shard_map/upd_first/pallas_call | solution.py:289
  821.8 8.7 %put_a.1.refs_6_ = bf16[16,2048,768]{2,1,0:T(8,128)(2,1)} custom-call(bf16[2048,768]{1,0:T(8,128)(2,1)} %collective-permute-done.refs_0_, bf16[2048,768]{1,0:T(8,128)(2,1)} %collective-permute-done.13.refs_1_, bf16[1024,768]{1,0:T(8,128)(2,1)} %collective-permute-done.14.refs_2_, ...), custom_call_target="tpu_custom_call", output_to_operand_aliasing={{}: (4, {})} | custom-call | flops 1651507200 | bytes 22020096 | tf_op jit(solution)/shard_map/put_a/pallas_call | solution.py:262
  830.6 8.4 put_b.1
  (33 shorter events, 3.1 us)
Async XLA Ops:
  7.2 758.3 %all-gather.3.cloned.1.call-start = ((), (), s32[]{:S(2)}) async-start(), calls=%async_computation | async-start | bytes 11796480 | tf_op jit(solution)/shard_map/all_gather | solution.py:775
  7.2 8.1 copy-start
  513.0 280.3 %all-gather.5.cloned.1.call-start = ((), (), s32[]{:S(2)}) async-start(), calls=%async_computation.1 | async-start | bytes 11796480 | tf_op jit(solution)/shard_map/all_gather | solution.py:776
  540.3 123.7 %collective-permute-start.1 = (bf16[2048,768]{1,0:T(8,128)(2,1)}, bf16[2048,768]{1,0:T(8,128)(2,1)}, u32[]{:S(2)}, u32[]{:S(2)}) collective-permute-start(bf16[2048,768]{1,0:T(8,128)(2,1)} %fwd_a3.1.refs_9_), channel_id=1, source_target_pairs={{0,2},{1,3},{2,0},{3,1},{4,6},{5,7},{6,4},{7,5},{8,10},{9,11},{10,... | collective-permute-start | bytes 9437192 | tf_op jit(solution)/shard_map/ppermute | solution.py:761
  541.8 122.2 %collective-permute-start.2 = (bf16[2048,768]{1,0:T(8,128)(2,1)}, bf16[2048,768]{1,0:T(8,128)(2,1)}, u32[]{:S(2)}, u32[]{:S(2)}) collective-permute-start(bf16[2048,768]{1,0:T(8,128)(2,1)} %fwd_a3.1.refs_9_), channel_id=1, source_target_pairs={{0,1},{1,0},{2,3},{3,2},{4,5},{5,4},{6,7},{7,6},{8,9},{9,8},{10,11... | collective-permute-start | bytes 9437192 | tf_op jit(solution)/shard_map/ppermute | solution.py:758
  568.9 95.1 %collective-permute-start.3 = (bf16[2048,768]{1,0:T(8,128)(2,1)}, bf16[2048,768]{1,0:T(8,128)(2,1)}, u32[]{:S(2)}, u32[]{:S(2)}) collective-permute-start(bf16[2048,768]{1,0:T(8,128)(2,1)} %fwd_a4.1.refs_10_), channel_id=1, source_target_pairs={{0,1},{1,0},{2,3},{3,2},{4,5},{5,4},{6,7},{7,6},{8,9},{9,8},{10,11... | collective-permute-start | bytes 9437192 | tf_op jit(solution)/shard_map/ppermute | solution.py:758
  569.5 144.9 %collective-permute-start = (bf16[2048,768]{1,0:T(8,128)(2,1)}, bf16[2048,768]{1,0:T(8,128)(2,1)}, u32[]{:S(2)}, u32[]{:S(2)}) collective-permute-start(bf16[2048,768]{1,0:T(8,128)(2,1)} %fwd_a4.1.refs_10_), channel_id=1, source_target_pairs={{0,2},{1,3},{2,0},{3,1},{4,6},{5,7},{6,4},{7,5},{8,10},{9,11},{10,... | collective-permute-start | bytes 9437192 | tf_op jit(solution)/shard_map/ppermute | solution.py:761
  664.0 51.3 %collective-permute-start.7 = (bf16[2048,768]{1,0:T(8,128)(2,1)}, bf16[2048,768]{1,0:T(8,128)(2,1)}, u32[]{:S(2)}, u32[]{:S(2)}) collective-permute-start(bf16[2048,768]{1,0:T(8,128)(2,1)} %get-tuple-element.85), channel_id=1, source_target_pairs={{0,1},{1,0},{2,3},{3,2},{4,5},{5,4},{6,7},{7,6},{8,9},{9,8},{10,11... | collective-permute-start | bytes 9437192 | tf_op jit(solution)/shard_map/ppermute | solution.py:758
  664.1 129.0 %collective-permute-start.5 = (bf16[2048,768]{1,0:T(8,128)(2,1)}, bf16[2048,768]{1,0:T(8,128)(2,1)}, u32[]{:S(2)}, u32[]{:S(2)}) collective-permute-start(bf16[2048,768]{1,0:T(8,128)(2,1)} %get-tuple-element.85), channel_id=1, source_target_pairs={{0,2},{1,3},{2,0},{3,1},{4,6},{5,7},{6,4},{7,5},{8,10},{9,11},{10,... | collective-permute-start | bytes 9437192 | tf_op jit(solution)/shard_map/ppermute | solution.py:761
  665.6 49.7 %collective-permute-start.6 = (bf16[2048,768]{1,0:T(8,128)(2,1)}, bf16[2048,768]{1,0:T(8,128)(2,1)}, u32[]{:S(2)}, u32[]{:S(2)}) collective-permute-start(bf16[2048,768]{1,0:T(8,128)(2,1)} %collective-permute-done.1.refs_9_), channel_id=1, source_target_pairs={{0,1},{1,0},{2,3},{3,2},{4,5},{5,4},{6,7},{7,6},{8,9},{9,8},{10,11... | collective-permute-start | bytes 9437192 | tf_op jit(solution)/shard_map/ppermute | solution.py:758
  714.4 107.0 %collective-permute-start.14 = (bf16[1024,768]{1,0:T(8,128)(2,1)}, bf16[1024,768]{1,0:T(8,128)(2,1)}, u32[]{:S(2)}, u32[]{:S(2)}) collective-permute-start(bf16[1024,768]{1,0:T(8,128)(2,1)} %get-tuple-element.84), channel_id=1, source_target_pairs={{0,1},{1,0},{2,3},{3,2},{4,5},{5,4},{6,7},{7,6},{8,9},{9,8},{10,11... | collective-permute-start | bytes 4718600 | tf_op jit(solution)/shard_map/ppermute | solution.py:758
  714.8 106.1 %collective-permute-start.4 = (bf16[1024,768]{1,0:T(8,128)(2,1)}, bf16[1024,768]{1,0:T(8,128)(2,1)}, u32[]{:S(2)}, u32[]{:S(2)}) collective-permute-start(bf16[1024,768]{1,0:T(8,128)(2,1)} %get-tuple-element.84), channel_id=1, source_target_pairs={{0,2},{1,3},{2,0},{3,1},{4,6},{5,7},{6,4},{7,5},{8,10},{9,11},{10,... | collective-permute-start | bytes 4718600 | tf_op jit(solution)/shard_map/ppermute | solution.py:761
  715.3 106.5 %collective-permute-start.13 = (bf16[2048,768]{1,0:T(8,128)(2,1)}, bf16[2048,768]{1,0:T(8,128)(2,1)}, u32[]{:S(2)}, u32[]{:S(2)}) collective-permute-start(bf16[2048,768]{1,0:T(8,128)(2,1)} %collective-permute-done.refs_0_), channel_id=1, source_target_pairs={{0,1},{1,0},{2,3},{3,2},{4,5},{5,4},{6,7},{7,6},{8,9},{9,8},{10,11... | collective-permute-start | bytes 9437192 | tf_op jit(solution)/shard_map/ppermute | solution.py:758
  763.9 57.4 %collective-permute-start.11 = (bf16[1024,768]{1,0:T(8,128)(2,1)}, bf16[1024,768]{1,0:T(8,128)(2,1)}, u32[]{:S(2)}, u32[]{:S(2)}) collective-permute-start(bf16[1024,768]{1,0:T(8,128)(2,1)} %get-tuple-element.104), channel_id=1, source_target_pairs={{0,2},{1,3},{2,0},{3,1},{4,6},{5,7},{6,4},{7,5},{8,10},{9,11},{10,... | collective-permute-start | bytes 4718600 | tf_op jit(solution)/shard_map/ppermute | solution.py:761
  793.1 37.5 %collective-permute-start.8 = (bf16[2048,768]{1,0:T(8,128)(2,1)}, bf16[2048,768]{1,0:T(8,128)(2,1)}, u32[]{:S(2)}, u32[]{:S(2)}) collective-permute-start(bf16[2048,768]{1,0:T(8,128)(2,1)} %collective-permute-done.5.refs_3_), channel_id=1, source_target_pairs={{0,1},{1,0},{2,3},{3,2},{4,5},{5,4},{6,7},{7,6},{8,9},{9,8},{10,11... | collective-permute-start | bytes 9437192 | tf_op jit(solution)/shard_map/ppermute | solution.py:758
  820.9 9.6 %collective-permute-start.10 = (bf16[1024,768]{1,0:T(8,128)(2,1)}, bf16[1024,768]{1,0:T(8,128)(2,1)}, u32[]{:S(2)}, u32[]{:S(2)}) collective-permute-start(bf16[1024,768]{1,0:T(8,128)(2,1)} %get-tuple-element.104), channel_id=1, source_target_pairs={{0,1},{1,0},{2,3},{3,2},{4,5},{5,4},{6,7},{7,6},{8,9},{9,8},{10,11... | collective-permute-start | bytes 4718600 | tf_op jit(solution)/shard_map/ppermute | solution.py:758
  821.3 9.3 %collective-permute-start.12 = (bf16[1024,768]{1,0:T(8,128)(2,1)}, bf16[1024,768]{1,0:T(8,128)(2,1)}, u32[]{:S(2)}, u32[]{:S(2)}) collective-permute-start(bf16[1024,768]{1,0:T(8,128)(2,1)} %collective-permute-done.11.refs_4_), channel_id=1, source_target_pairs={{0,1},{1,0},{2,3},{3,2},{4,5},{5,4},{6,7},{7,6},{8,9},{9,8},{10,11... | collective-permute-start | bytes 4718600 | tf_op jit(solution)/shard_map/ppermute | solution.py:758
  821.5 9.1 %collective-permute-start.9 = (bf16[1024,768]{1,0:T(8,128)(2,1)}, bf16[1024,768]{1,0:T(8,128)(2,1)}, u32[]{:S(2)}, u32[]{:S(2)}) collective-permute-start(bf16[1024,768]{1,0:T(8,128)(2,1)} %collective-permute-done.4.refs_1_), channel_id=1, source_target_pairs={{0,1},{1,0},{2,3},{3,2},{4,5},{5,4},{6,7},{7,6},{8,9},{9,8},{10,11... | collective-permute-start | bytes 4718600 | tf_op jit(solution)/shard_map/ppermute | solution.py:758
Sparse Core Ops, SparseCore 0:
  513.1 91.9 all-gather.2
  606.9 92.3 all-gather.4

commit v2 on v1

--- a/solution.py
+++ b/solution.py
@@ -62,28 +62,31 @@
     return half + half * jnp.tanh(z * (ROOT + ROOT * CUBE * (z * z)))
 
 
-def forward_kernel(n_blk, spec, n_side, side_rows, gather, *refs):
+def mlp_tile(x_buf, rows, w_v, h_buf):
+    x = x_buf[rows, :]
+    for j in range(4):
+        z = jnp.dot(x, w_v[j, 0], preferred_element_type=F32)
+        h_buf[:, j * DIM:(j + 1) * DIM] = gelu_kernel(z).astype(BF16)
+    acc = jnp.dot(h_buf[...], jnp.concatenate([w_v[j, 1] for j in range(4)], 0), preferred_element_type=F32)
+    x_buf[rows, :] = (x.astype(F32) + acc).astype(BF16)
+
+
+def forward_kernel(blocks, spec, n_side, side_rows, *refs):
     in_next, first_group, row0, n_rows, to_out, has_out_in = spec
     refs = list(refs)
     ends = [sum(k[-1] for k in side_rows[:i]) for i in range(n_side)]
     x_ref = refs.pop(0)
-    w_refs = [(refs.pop(0), refs.pop(0)) for _ in range(n_blk)]
-    q_ref = refs.pop(0) if gather else None
+    w_ref = refs.pop(0)
+    n_blk = len(blocks)
     side_refs = [refs.pop(0) for _ in range(n_side)]
     if has_out_in:
         refs.pop(0)
     if to_out:
         out_ref = refs.pop(0)
     y_ref = refs.pop(0)
-    gathered = [refs.pop(0) for _ in range(2)] if gather else None
     w_buf, x_buf, h_buf, w_sem, x_sem, y_sem, o_sem = refs[:7]
     bounce = refs[7:]
-    steps = None
-    if gather:
-        z_v, m_v = bounce[:2]
-        steps = exchange_steps(lambda part: q_ref.at[part], z_v, m_v, bounce[2:9])
     stage = lax.axis_index('stage')
-    core = lax.rem(stage, 2)
     n_tiles = n_rows // TILE
     n_mb = max(1, n_rows // ROWS)
     mb_rows = n_rows // n_mb
@@ -97,14 +100,10 @@
                 x_buf.at[pl.ds(q * mb_rows, mb_rows)], x_sem.at[q])
             for q in range(n_mb)]
 
-    def w_copies(blk):
-        own = pl.multiple_of(core * HALF, HALF)
-        mate = pl.multiple_of((1 - core) * HALF, HALF)
-        return [
-            pltpu.make_async_copy(w_refs[blk][0], w_buf.at[blk, :, :, pl.ds(own, HALF)], w_sem.at[blk, 0]),
-            pltpu.make_async_copy(w_refs[blk][1], w_buf.at[blk, :, :, pl.ds(mate, HALF)], w_sem.at[blk, 1])]
-
-    for cp in x_copies() + w_copies(0):
+    def w_copy(blk):
+        return pltpu.make_async_copy(w_ref.at[blocks[0] + blk], w_buf.at[blk], w_sem.at[blk])
+
+    for cp in x_copies() + [w_copy(0)]:
         cp.start()
     for cp in x_copies():
         cp.wait()
@@ -128,13 +127,11 @@
         return pltpu.make_async_copy(x_buf.at[pl.ds(pl.multiple_of(t * TILE, TILE), TILE)], out_ref.at[4 * first_group + stage, pl.ds(row0 + pl.multiple_of(t * TILE, TILE), TILE)], o_sem.at[t])
 
     def blk_body(blk, _):
-        for half in range(2):
-            pltpu.make_async_copy(w_buf.at[blk, :, :, pl.ds(0, HALF)], w_buf.at[blk, :, :, pl.ds(0, HALF)], w_sem.at[blk, half]).wait()
-        for nxt in range(1, n_blk):
-            @pl.when(blk == nxt - 1)
-            def _():
-                for cp in w_copies(nxt):
-                    cp.start()
+        w_copy(blk).wait()
+
+        @pl.when(blk < n_blk - 1)
+        def _():
+            w_copy(blk + 1).start()
 
         if n_side:
             @pl.when(blk == 0)
@@ -151,15 +148,7 @@
 
         def tile_body(t, _):
             rows = pl.ds(pl.multiple_of(t * TILE, TILE), TILE)
-            if gather:
-                for when, step in ((0, 0), (3, 1), (5, 2), (7, 3)):
-                    pl.when(t == when)(steps[step])
-            x = x_buf[rows, :]
-            for j in range(4):
-                z = jnp.dot(x, w_buf[blk, j, 0], preferred_element_type=F32)
-                h_buf[:, j * DIM:(j + 1) * DIM] = gelu_kernel(z).astype(BF16)
-            acc = jnp.dot(h_buf[...], jnp.concatenate([w_buf[blk, j, 1] for j in range(4)], 0), preferred_element_type=F32)
-            x_buf[rows, :] = (x.astype(F32) + acc).astype(BF16)
+            mlp_tile(x_buf, rows, w_buf.at[blk], h_buf)
 
             @pl.when(jnp.logical_and(blk == n_blk - 1, t > 0))
             def _():
@@ -174,14 +163,6 @@
     y_copy(n_tiles - 1).start()
     if to_out:
         o_copy(n_tiles - 1).start()
-    if gather:
-        keep = [pltpu.make_async_copy(z_v, gathered[0], bounce[9].at[0]), pltpu.make_async_copy(m_v, gathered[1], bounce[9].at[1])]
-        keep[0].start()
-        steps[4]()
-        keep[1].start()
-        steps[5]()
-        for cp in keep:
-            cp.wait()
     for t in range(n_tiles):
         y_copy(t).wait()
         if to_out:
@@ -190,43 +171,38 @@
         side_out(i).wait()
 
 
-def run_forward(x, weights, chunk, name, to_out=False, out_buf=None, sides=(), piece=None):
+def run_forward(x, weights, chunk, name, to_out=False, out_buf=None, sides=(), blocks=(0, 1, 2, 3)):
     n_rows = chunk[-1]
     in_next = x.ndim > 2
     has_out_in = out_buf is not None
     side_rows = [(flip,) + where for _, flip, where in sides]
     sides = [rows for rows, _, _ in sides]
     spec = (in_next,) + chunk + (to_out, has_out_in)
-    n_blk = len(weights)
+    n_blk = len(blocks)
     n_tiles = n_rows // TILE
-    args = [x] + [w for pair in weights for w in pair] + ([piece] if piece is not None else []) + list(sides) + ([out_buf] if has_out_in else [])
+    args = [x, weights] + list(sides) + ([out_buf] if has_out_in else [])
     shapes, alias = [], {}
     if to_out:
         shapes.append(jax.ShapeDtypeStruct((16, ROWS, DIM), BF16))
         if has_out_in:
             alias = {len(args) - 1: 0}
     shapes.append(jax.ShapeDtypeStruct((n_rows, DIM), BF16))
-    gather = piece is not None
-    if gather:
-        shapes += [jax.ShapeDtypeStruct((4, 2, HALF, DIM), BF16)] * 2
     scratch = [
         pltpu.VMEM((n_blk, 4, 2, DIM, DIM), BF16),
         pltpu.VMEM((n_rows, DIM), BF16),
         pltpu.VMEM((TILE, FFN), BF16),
-        DMA((n_blk, 2)),
+        DMA((n_blk,)),
         DMA((2,)),
         ] + [DMA((n_tiles,))] * 2
-    if gather:
-        scratch += EXCHANGE_BUFS + EXCHANGE_SEMS + [DMA((2,))]
     if sides:
         scratch += [pltpu.VMEM((sum(k[-1] for k in side_rows), DIM), BF16), DMA((len(sides),)), DMA((len(sides),))]
     flops = n_rows * n_blk * 4 * DIM * FFN
     res = pl.pallas_call(
-        functools.partial(forward_kernel, n_blk, spec, len(sides), tuple(side_rows), gather),
+        functools.partial(forward_kernel, tuple(blocks), spec, len(sides), tuple(side_rows)),
         out_shape=shapes, in_specs=[ANY] * len(args), out_specs=[ANY] * len(shapes),
         scratch_shapes=scratch, input_output_aliases=alias, name=name,
         cost_estimate=pl.CostEstimate(flops=flops, bytes_accessed=n_blk * 9 * MIB + n_rows * FFN, transcendentals=n_rows * n_blk * FFN),
-        compiler_params=pltpu.CompilerParams(vmem_limit_bytes=VMEM_BIG, has_side_effects=gather),
+        compiler_params=pltpu.CompilerParams(vmem_limit_bytes=VMEM_BIG),
     )(*args)
     return res if len(res) > 1 else res[0]
 
@@ -305,24 +281,29 @@
     return pltpu.make_async_remote_copy(src_ref=src, dst_ref=dst, send_sem=send_sem, recv_sem=recv_sem, device_id=(data, stage), device_id_type=MESH_ID)
 
 
-def exchange_steps(own, z_v, m_v, sems, before=None):
+def exchange_steps(own, w_v, sems, before=None):
     ys, yr, zs, zr, ms, mr, ls = sems
-    stage, _, rep, mate, near = ids()
+    stage, core, rep, mate, near = ids()
+    mine = pl.ds(pl.multiple_of(core * HALF, HALF), HALF)
+
+    def z_at(quarter, part):
+        return w_v.at[quarter, part, mine, :]
+
     y_id, z_id, d_id = near[1:]
 
     def over_y(src, quarter, part, i):
-        return push(src, z_v.at[quarter, part], ys.at[i], yr.at[i], y_id, stage)
+        return push(src, z_at(quarter, part), ys.at[i], yr.at[i], y_id, stage)
 
     def over_z(src, quarter, part, i):
-        return push(src, z_v.at[quarter, part], zs.at[i], zr.at[i], z_id, stage)
+        return push(src, z_at(quarter, part), zs.at[i], zr.at[i], z_id, stage)
 
     def cross(quarter, part, src=None):
         i = quarter * 2 + part
-        src = z_v.at[quarter, part] if src is None else src
-        return push(src, m_v.at[quarter, part], ms.at[i], mr.at[i], rep, mate)
+        src = z_at(quarter, part) if src is None else src
+        return push(src, z_at(quarter, part), ms.at[i], mr.at[i], rep, mate)
 
     def local(part):
-        return pltpu.make_async_copy(own(part), z_v.at[rep, part], ls.at[part])
+        return pltpu.make_async_copy(own(part), z_at(rep, part), ls.at[part])
 
     def start():
         for part in (FIRST, SECOND):
@@ -335,14 +316,14 @@
 
     def first():
         over_y(own(FIRST), y_id, FIRST, FIRST).wait_recv()
-        over_z(z_v.at[y_id, FIRST], y_id, FIRST, SUMS).start()
+        over_z(z_at(y_id, FIRST), y_id, FIRST, SUMS).start()
         cross(y_id, FIRST).start()
         over_z(own(FIRST), z_id, FIRST, FIRST).wait_recv()
         cross(z_id, FIRST).start()
 
     def second():
         over_z(own(SECOND), z_id, SECOND, SECOND).wait_recv()
-        over_y(z_v.at[z_id, SECOND], z_id, SECOND, SUMS).start()
+        over_y(z_at(z_id, SECOND), z_id, SECOND, SUMS).start()
         cross(z_id, SECOND).start()
         over_y(own(SECOND), y_id, SECOND, SECOND).wait_recv()
         cross(y_id, SECOND).start()
@@ -371,8 +352,7 @@
     return start, first, second, third, last, drain
 
 
-EXCHANGE_SEMS = [DMA((3,))] * 4 + [DMA((8,))] * 2 + [DMA((2,))]
-EXCHANGE_BUFS = [pltpu.VMEM((4, 2, HALF, DIM), BF16)] * 2
+EXCHANGE_SEMS = [DMA((4, 3))] * 4 + [DMA((4, 8)), DMA((4, 8)), DMA((4, 2))]
 
 
 def reduce_kernel(h_ref, g_ref, a_ref, p_ref, acc2_ref, acc1_ref, r2_ref, r1_ref,
@@ -493,18 +473,22 @@
 N_CHUNK = 8
 
 
-def backward_kernel(a_ref, d_ref, w1_ref, w2_ref, h_ref, dz_ref, g_ref, a_v, w1_v, w2_v, z_v, g_v, h_b, p_b, s_b,
-                    in_sem, h_sem, p_sem, o_sem, send_sem, recv_sem):
+def backward_kernel(a_ref, d_ref, w1_ref, w2_ref, h_ref, dz_ref, g_ref, a_v, w1_v, w2_v, c_v, z_v, g_v, h_b, p_b, s_b,
+                    in_sem, w_sem, h_sem, p_sem, o_sem, send_sem, recv_sem):
     stage = lax.axis_index('stage')
     rep = lax.axis_index('data')
     rows = a_v.shape[0] // N_CHUNK
     below = jnp.maximum(stage - 1, 0)
     cp_a = pltpu.make_async_copy(a_ref.at[0], a_v, in_sem.at[0])
-    cp_1 = pltpu.make_async_copy(w1_ref, w1_v, in_sem.at[1])
-    cp_2 = pltpu.make_async_copy(w2_ref, w2_v, in_sem.at[2])
     cp_a.start()
-    cp_1.start()
-    cp_2.start()
+
+    def w_copy(i):
+        span = pl.ds((i % 4) * DIM, DIM)
+        src = w1_ref.at[0, :, span] if i < 4 else w2_ref.at[0, span, :]
+        return pltpu.make_async_copy(src, c_v.at[i % 3], w_sem.at[i])
+
+    for i in range(3):
+        w_copy(i).start()
     n_pre = jnp.where(stage == 3, 0, jnp.where(stage == 2, 4, N_CHUNK))
 
     def d_copy(k):
@@ -546,10 +530,17 @@
         h_copy(k).start()
         return 0
 
+    for i in range(8):
+        w_copy(i).wait()
+        span = slice((i % 4) * DIM, (i % 4 + 1) * DIM)
+        if i < 4:
+            w1_v[:, span] = c_v[i % 3].astype(BF16)
+        else:
+            w2_v[span, :] = c_v[i % 3].astype(BF16)
+        if i < 5:
+            w_copy(i + 3).start()
     cp_a.wait()
-    cp_1.wait()
     lax.fori_loop(0, n_pre, z_body, 0)
-    cp_2.wait()
 
     def chain_body(k, _):
         lax.fori_loop(k, jnp.where(k >= n_pre, k + 1, k), z_body, 0)
@@ -602,78 +593,89 @@
         backward_kernel, in_specs=[ANY] * 4, out_specs=[ANY] * 3, name='backward',
         out_shape=[jax.ShapeDtypeStruct((n, FFN), BF16), jax.ShapeDtypeStruct((n, FFN), BF16), jax.ShapeDtypeStruct((n, DIM), BF16)],
         scratch_shapes=[
-            pltpu.VMEM((n, DIM), BF16), pltpu.VMEM((DIM, FFN), BF16), pltpu.VMEM((FFN, DIM), BF16),
+            pltpu.VMEM((n, DIM), BF16), pltpu.VMEM((DIM, FFN), BF16), pltpu.VMEM((FFN, DIM), BF16), pltpu.VMEM((3, DIM, DIM), F32),
             pltpu.VMEM((N_CHUNK, rows, FFN), F32), pltpu.VMEM((N_CHUNK, rows, DIM), BF16),
             pltpu.VMEM((2, rows, FFN), BF16), pltpu.VMEM((2, rows, FFN), BF16), pltpu.VMEM((N_CHUNK, rows, DIM), BF16),
-            DMA((3,)), DMA((N_CHUNK,)), DMA((N_CHUNK,)),
+            DMA((1,)), DMA((8,)), DMA((N_CHUNK,)), DMA((N_CHUNK,)),
             DMA((N_CHUNK,)), DMA((N_CHUNK,)), DMA((N_CHUNK,))],
         cost_estimate=pl.CostEstimate(flops=6 * n * DIM * FFN, bytes_accessed=50_000_000, transcendentals=2 * n * FFN),
         compiler_params=pltpu.CompilerParams(vmem_limit_bytes=VMEM_BIG, has_side_effects=True),
     )(acts, d_out, w1, w2)
 
 
-def middle_kernel(lr_ref, mx_ref, r1_ref, r2_ref, w1_ref, m1_ref, v1_ref, w2_ref, m2_ref, v2_ref,
-                  own_ref, mate_ref, q1_ref, q2_ref, q3_ref, scal_ref,
-                  p_v, q_v, z_v, m_v, s_v, n_v, in_sem, ns, nr, hs, hr, xs, xr, o_sem, *sems):
-    stage = lax.axis_index('stage')
-    rep = lax.axis_index('data')
-    core = lax.rem(stage, 2)
+def middle_kernel(lr_ref, mx_ref, r1_ref, r2_ref, w1_ref, m1_ref, v1_ref, w2_ref, m2_ref, v2_ref, x_ref,
+                  y_ref, all_ref, scal_ref, r_v, p_v, q_v, s_v, n_v, w_v, x_buf, h_buf,
+                  r_sem, p_sem, x_sem, ns, nr, hs, hr, xs, xr, o_sem, y_sem, *sems):
+    stage, core, rep, mate, _ = ids()
     side = lax.div(stage, 2)
     base = 2 * side
+    far = lax.rem(stage + 2, 4)
     me = rep * 4 + stage
-
-    cols = pl.ds(pl.multiple_of(rep * DIM, DIM), DIM)
-    srcs = [r1_ref.at[0], r2_ref.at[0], w1_ref.at[0, :, cols], m1_ref.at[0, :, cols], v1_ref.at[0, :, cols],
-            w2_ref.at[0, cols, :], m2_ref.at[0, cols, :], v2_ref.at[0, cols, :]]
-    loads = [pltpu.make_async_copy(srcs[i], p_v.at[i], in_sem.at[i]) for i in range(8)]
-    for cp in loads:
+    n_dev = 16
+    n_tile = x_buf.shape[0] // TILE
+
+    r_loads = [pltpu.make_async_copy(ref.at[0], r_v.at[k], r_sem.at[k]) for k, ref in enumerate((r1_ref, r2_ref))]
+
+    def loads(turn, k):
+        half = (1 - core) if turn == 0 else core
+        start = pl.multiple_of(rep * DIM, DIM)
+        if k == 0:
+            refs, where = (w1_ref, m1_ref, v1_ref), (0, pl.ds(pl.multiple_of(half * HALF, HALF), HALF), pl.ds(start, DIM))
+        else:
+            refs, where = (w2_ref, m2_ref, v2_ref), (0, pl.ds(pl.multiple_of(start + half * HALF, HALF), HALF))
+        return [pltpu.make_async_copy(ref.at[where], p_v.at[k, i], p_sem.at[turn, k, i]) for i, ref in enumerate(refs)]
+
+    x_loads = [pltpu.make_async_copy(x_ref.at[4 * q + stage], x_buf.at[pl.ds(q * ROWS, ROWS)], x_sem.at[q]) for q in range(2)]
+    for cp in r_loads + loads(0, 0) + loads(0, 1) + x_loads:
         cp.start()
-    loads[0].wait()
-    loads[1].wait()
+    for cp in r_loads:
+        cp.wait()
 
     def sq_body(t, acc):
-        rows = pl.ds(pl.multiple_of(t * 64, 64), 64)
-        a = p_v[0, rows, :]
-        b = p_v[1, rows, :]
+        rows = pl.ds(pl.multiple_of(t * STRIP, STRIP), STRIP)
+        a = r_v[0, rows, :]
+        b = r_v[1, rows, :]
         return acc + a * a + b * b
-    acc = lax.fori_loop(0, 12, sq_body, jnp.zeros((64, DIM), F32))
-    n_v[me] = jnp.full((8, 128), jnp.sum(acc), F32)
-
-    def norm_send(i, peer):
+    acc = lax.fori_loop(0, DIM // STRIP, sq_body, jnp.zeros((STRIP, DIM), F32))
+    n_v[me] = jnp.full(n_v.shape[1:], jnp.sum(acc), F32)
+
+    def norm_send(i):
+        peer = lax.rem(me + i, n_dev)
         return push(n_v.at[me], n_v.at[me], ns.at[i], nr.at[i], lax.div(peer, 4), lax.rem(peer, 4))
 
-    def peer_of(i):
-        return lax.rem(me + i, 16)
-
-    for i in range(1, 16):
-        norm_send(i, peer_of(i)).start()
-    for i in range(1, 16):
-        norm_send(i, peer_of(i)).wait()
+    for i in range(1, n_dev):
+        norm_send(i).start()
+    for i in range(1, n_dev):
+        norm_send(i).wait()
     total = n_v[0]
-    for i in range(1, 16):
+    for i in range(1, n_dev):
         total = total + n_v[i]
-    norm = jnp.sqrt(total[0:1, 0:1] * 0.0625)
+    norm = jnp.sqrt(total[:1, :1] * 0.0625)
     clip = jnp.minimum(1.0, mx_ref[0] / (norm + NORM_EPS)) * 0.25
-    scal_ref[...] = jnp.broadcast_to(clip, (8, 128))
-    for cp in loads[2:]:
-        cp.wait()
+    scal_ref[...] = jnp.broadcast_to(clip, scal_ref.shape)
     lr = lr_ref[0]
 
-    def upd(half, dst):
+    def upd(turn, dst):
+        half = (1 - core) if turn == 0 else core
         for k in range(2):
+            for cp in loads(turn, k):
+                cp.wait()
+
             def body(t, _):
-                rows = pl.ds(pl.multiple_of(half * HALF + t * 64, 64), 64)
-                new = adamw_update(p_v[2 + 3 * k, rows, :], p_v[3 + 3 * k, rows, :], p_v[4 + 3 * k, rows, :], p_v[k, rows, :], clip, lr)[0]
-                dst[k, pl.ds(pl.multiple_of(t * 64, 64), 64), :] = new.astype(BF16)
+                here = pl.ds(pl.multiple_of(t * STRIP, STRIP), STRIP)
+                rows = pl.ds(pl.multiple_of(half * HALF + t * STRIP, STRIP), STRIP)
+                new = adamw_update(p_v[k, 0, here, :], p_v[k, 1, here, :], p_v[k, 2, here, :], r_v[k, rows, :], clip, lr)[0]
+                dst[k, here, :] = new.astype(BF16)
                 return 0
-            lax.fori_loop(0, 6, body, 0)
-
-    mate = base + 1 - core
-    far = lax.rem(stage + 2, 4)
-    upd(1 - core, s_v)
+            lax.fori_loop(0, HALF // STRIP, body, 0)
+            if turn == 0:
+                for cp in loads(1, k):
+                    cp.start()
+
+    upd(0, s_v)
     half_cp = push(s_v, q_v.at[stage], hs, hr, rep, mate)
     half_cp.start()
-    upd(core, q_v.at[stage])
+    upd(1, q_v.at[stage])
     half_cp.wait_send()
     push(s_v, q_v.at[mate], hs, hr, rep, mate).wait_recv()
 
@@ -691,10 +693,12 @@
         def _():
             x_in[part].wait_recv()
 
-    steps = exchange_steps(lambda part: q_v.at[0, part], z_v, m_v, sems, before)
-    for step in steps[:4]:
+    def steps_of(blk, hook=None):
+        slot = lax.rem(blk, 3)
+        return exchange_steps(lambda part: q_v.at[blk, part], w_v.at[slot], [sem.at[blk] for sem in sems], hook)
+
+    for step in steps_of(0, before):
         step()
-    outs = [pltpu.make_async_copy(z_v, own_ref, o_sem.at[0])]
 
     @pl.when(side == 0)
     def _():
@@ -702,33 +706,60 @@
         x_in[1].wait_recv()
     x_in[2].wait_recv()
     x_in[3].wait_recv()
-    outs += [pltpu.make_async_copy(q_v.at[b], r, o_sem.at[b]) for b, r in enumerate((q1_ref, q2_ref, q3_ref), 1)]
-    for cp in outs:
-        cp.start()
-    steps[4]()
-    outs.append(pltpu.make_async_copy(m_v, mate_ref, o_sem.at[4]))
-    outs[4].start()
     for cp in x_out:
         cp.wait_send()
-    steps[5]()
-    for cp in outs:
+    for cp in x_loads:
         cp.wait()
 
-
-def run_middle(lr, mx, r1, r2, w1, m1, v1, w2, m2, v2):
+    def keep(blk):
+        return pltpu.make_async_copy(w_v.at[lax.rem(blk, 3)], all_ref.at[blk], o_sem.at[blk])
+
+    def y_copy(t):
+        rows = pl.ds(pl.multiple_of(t * TILE, TILE), TILE)
+        return pltpu.make_async_copy(x_buf.at[rows], y_ref.at[rows], y_sem.at[t])
+
+    def blk_body(blk, _):
+        keep(blk).start()
+        steps = steps_of(blk + 1)
+
+        def tile_body(t, _):
+            for when, step in zip((0, 3, 5, 7), steps):
+                pl.when(t == when)(step)
+            mlp_tile(x_buf, pl.ds(pl.multiple_of(t * TILE, TILE), TILE), w_v.at[blk], h_buf)
+
+            @pl.when(jnp.logical_and(blk == 2, t > 0))
+            def _():
+                y_copy(t - 1).start()
+            return 0
+        lax.fori_loop(0, n_tile, tile_body, 0)
+        for step in steps[4:]:
+            step()
+        keep(blk).wait()
+        return 0
+
+    lax.fori_loop(0, 3, blk_body, 0)
+    y_copy(n_tile - 1).start()
+    keep(3).start()
+    for t in range(n_tile):
+        y_copy(t).wait()
+    keep(3).wait()
+
+
+def run_middle(lr, mx, r1, r2, w1, m1, v1, w2, m2, v2, x):
     smem = pl.BlockSpec(memory_space=pltpu.SMEM)
-    piece = jax.ShapeDtypeStruct((2, HALF, DIM), BF16)
-    block = jax.ShapeDtypeStruct((4, 2, HALF, DIM), BF16)
+    n_rows = 2 * ROWS
     return pl.pallas_call(
-        middle_kernel, in_specs=[smem, smem] + [ANY] * 8,
-        out_specs=[ANY] * 5 + [pl.BlockSpec(memory_space=pltpu.VMEM)],
-        out_shape=[block, block, piece, piece, piece, jax.ShapeDtypeStruct((8, 128), F32)], name='middle',
+        middle_kernel, in_specs=[smem, smem] + [ANY] * 9,
+        out_specs=[ANY] * 2 + [pl.BlockSpec(memory_space=pltpu.VMEM)],
+        out_shape=[jax.ShapeDtypeStruct((n_rows, DIM), BF16), jax.ShapeDtypeStruct((4, 4, 2, DIM, DIM), BF16), jax.ShapeDtypeStruct((8, 128), F32)], name='middle',
         scratch_shapes=[
-            pltpu.VMEM((8, DIM, DIM), F32), pltpu.VMEM((4, 2, HALF, DIM), BF16)] + EXCHANGE_BUFS + [
-            pltpu.VMEM((2, HALF, DIM), BF16), pltpu.VMEM((16, 8, 128), F32), DMA((8,)), DMA((16,)), DMA((16,)), DMA, DMA, DMA((4,)), DMA((4,)), DMA((5,))] + EXCHANGE_SEMS,
-        cost_estimate=pl.CostEstimate(flops=60_000_000_000, bytes_accessed=40_000_000, transcendentals=0),
+            pltpu.VMEM((2, DIM, DIM), F32), pltpu.VMEM((2, 3, HALF, DIM), F32), pltpu.VMEM((4, 2, HALF, DIM), BF16),
+            pltpu.VMEM((2, HALF, DIM), BF16), pltpu.VMEM((16, 8, 128), F32), pltpu.VMEM((3, 4, 2, DIM, DIM), BF16),
+            pltpu.VMEM((n_rows, DIM), BF16), pltpu.VMEM((TILE, FFN), BF16),
+            DMA((2,)), DMA((2, 2, 3)), DMA((2,)), DMA((16,)), DMA((16,)), DMA, DMA, DMA((4,)), DMA((4,)), DMA((4,)), DMA((n_rows // TILE,))] + EXCHANGE_SEMS,
+        cost_estimate=pl.CostEstimate(flops=200_000_000_000, bytes_accessed=100 * MIB, transcendentals=0),
         compiler_params=pltpu.CompilerParams(vmem_limit_bytes=VMEM_BIG, has_side_effects=True),
-    )(lr, mx, r1, r2, w1, m1, v1, w2, m2, v2)
+    )(lr, mx, r1, r2, w1, m1, v1, w2, m2, v2, x)
 
 
 def solution(mesh):
@@ -737,22 +768,14 @@
     row_spec = P(None, 'data', None)
 
     def stage_program(w_in, w_out, mom_in, mom_out, var_in, var_out, acc_in, acc_out, stage_acts, d_out, next_x, learn_rate, max_norm):
-        w_first = w_in[0].astype(BF16)
-        w_second = w_out[0].astype(BF16)
-        act_h, pre_keep, grad_keep = run_backward(stage_acts, d_out, w_first, w_second)
+        act_h, pre_keep, grad_keep = run_backward(stage_acts, d_out, w_in, w_out)
         sh_second, sh_first = run_reduce(act_h, grad_keep, stage_acts, pre_keep, acc_out, acc_in)
-        own, mate, piece1, piece2, piece3, scal = run_middle(learn_rate, max_norm, sh_first, sh_second, w_in, mom_in, var_in, w_out, mom_out, var_out)
+        rows_a, weights, scal = run_middle(learn_rate, max_norm, sh_first, sh_second, w_in, mom_in, var_in, w_out, mom_out, var_out, next_x)
         scal = jnp.stack([scal[0, 0], learn_rate[0]])
-        weights = [(own, mate)]
-        rows_a = next_x
-        both = CHUNK_0[:-1] + (2 * ROWS,)
-        for blk, piece in enumerate((piece1, piece2, piece3)):
-            rows_a, own, mate = run_forward(rows_a, weights[blk:], both, f'fwd_a{blk}', piece=piece)
-            weights.append((own, mate))
         sh_second, sh_first, rows_a = lax.optimization_barrier((sh_second, sh_first, rows_a))
-        y_0 = run_forward(rows_a, weights[-1:], CHUNK_0, 'fwd_a3')
+        y_0 = run_forward(rows_a, weights, CHUNK_0, 'fwd_a3', blocks=(3,))
         rows_a, y_0 = lax.optimization_barrier((rows_a, y_0))
-        y_1 = run_forward(rows_a, weights[-1:], CHUNK_0[:1] + (ROWS, ROWS), 'fwd_a4')
+        y_1 = run_forward(rows_a, weights, CHUNK_0[:1] + (ROWS, ROWS), 'fwd_a4', blocks=(3,))
 
         def to_mate(rows):
             return lax.ppermute(rows, 'stage', CORE_PERM)

time: 853 us -> 812 us (0.952)
  Pallas kernels: 809 us -> 774 us
  other arithmetic: 10.9 us -> 1.26 us
    pallas_call x9 -> x6, Pallas kernels: 496 us -> 458 us  [the longest x5 243 us: run_forward(): pl.pallas_call(functools.partial(forward_kernel, tuple(blocks), spec, len...]
    convert_element_type x2 -> x0, other arithmetic: 9.58 us -> none  [the longest x1 6.69 us: stage_program(): w_second = w_out[0].astype(BF16)]
  transfers between devices with their start and end apart: 17 -> 17, of which waited for: 0 -> 0; matrix products, arithmetic and copies ran while one was open for 0% -> 0% of each run, Pallas kernels for 36% -> 38%
where the time goes in v2:
time: 812 us; the launch traced here: 806 us
  Pallas kernels  774 us (95%)
  between operations  16 us (2%)
  starting transfers between devices  13 us (2%)
    pallas_call x5, Pallas kernels, run_forward(): pl.pallas_call(functools.partial(forward_kernel, tuple(blocks), spec, len...  243 us
    pallas_call x1, Pallas kernels, run_middle(): pl.pallas_call(middle_kernel, in_specs=[smem, smem] + [ANY] * 9, out_spec...  215 us
    pallas_call x1, Pallas kernels, run_reduce(): pl.pallas_call(reduce_kernel, in_specs=[ANY] * 6, out_specs=[ANY] * 2, ou...  166 us
    pallas_call x1, Pallas kernels, run_backward(): pl.pallas_call(backward_kernel, in_specs=[ANY] * 4, out_specs=[ANY] * 3,...  77.6 us
    pallas_call x2, Pallas kernels, run_update(): pl.pallas_call(update_kernel, grid=grid, in_specs=[pl.BlockSpec(memory_sp...  55.2 us
    pallas_call x2, Pallas kernels, run_copy(): pl.pallas_call(functools.partial(copy_kernel, n_side, tuple(side_rows)),...  17.2 us
  transfers between devices with their start and end apart: 17, of which 0 were waited for; matrix products, arithmetic and copies ran while one was open for 0% of the time, Pallas kernels for 38%

profile of v2, /device:TPU:0, one launch (start us, length us, event | category | flops | bytes accessed | tf_op | source)
XLA Modules:
  0.0 805.6 jit_solution(11898705150499266932)
XLA Ops:
  8.5 77.6 %backward.1 = (bf16[2048,3072]{1,0:T(8,128)(2,1)}, bf16[2048,3072]{1,0:T(8,128)(2,1)}, bf16[2048,768]{1,0:T(8,128)(2,1)}) custom-call(bf16[1,2048,768]{2,1,0:T(8,128)(2,1)} %a_ref.3, bf16[2048,768]{1,0:T(8,128)(2,1)} %d_ref.1, f32[1,768,3072]{2,1,0:T(8,128)} %w_ref.3, f32[1,3072,768]{2,1,0:T(8,128)} %w_ref.2), custom_call_target="tpu_custom_call" | custom-call | flops 28991029248 | bytes 50000000 | tf_op jit(solution)/shard_map/backward/pallas_call | solution.py:592
  86.1 166.5 %reduce.1 = (f32[1,768,768]{2,1,0:T(8,128)}, f32[1,768,768]{2,1,0:T(8,128)}) custom-call(bf16[2048,3072]{1,0:T(8,128)(2,1)} %get-tuple-element.45.h_ref, bf16[2048,768]{1,0:T(8,128)(2,1)} %get-tuple-element.46.g_ref, bf16[1,2048,768]{2,1,0:T(8,128)(2,1)} %a_ref.3, bf16[2048,3072]{1,0:T(8,128)(2,1)} %get-tuple-element.47.p_ref, f32[1,1,3072,768]{3,2,1,0:T(8,128)} %acc2_ref.1, ...), custom_call_target="tpu_custom_call" | custom-call | flops 149999992832 | bytes 73400320 | tf_op jit(solution)/shard_map/reduce/pallas_call | solution.py:457
  252.6 214.9 %middle.1 = (bf16[4096,768]{1,0:T(8,128)(2,1)}, bf16[4,4,2,768,768]{4,3,2,1,0:T(8,128)(2,1)}, f32[8,128]{1,0:T(8,128)}) custom-call(f32[1]{0:T(128)S(6)} %copy.28.lr_ref, f32[1]{0:T(128)S(6)} %copy.29.mx_ref, f32[1,768,768]{2,1,0:T(8,128)} %get-tuple-element.70.r1_ref, f32[1,768,768]{2,1,0:T(8,128)} %get-tuple-element.67.r2_ref, f32[1,768,3072]{2,1,0:T(8,128)} %w_ref.3, ...), custom_call_target="tpu_custom_call" | custom-call | flops 199999995904 | bytes 104857600 | tf_op jit(solution)/shard_map/middle/pallas_call | solution.py:751
  467.5 0.3 all-gather.5.cloned.1.call-start
  467.8 27.1 %fwd_a3.1.refs_2_ = bf16[2048,768]{1,0:T(8,128)(2,1)} custom-call(bf16[4096,768]{1,0:T(8,128)(2,1)} %get-tuple-element.53.refs_0_, bf16[4,4,2,768,768]{4,3,2,1,0:T(8,128)(2,1)} %get-tuple-element.52.refs_1_), custom_call_target="tpu_custom_call" | custom-call | flops 19327352832 | bytes 15728640 | tf_op jit(solution)/shard_map/fwd_a3/pallas_call | solution.py:200
  494.9 6.3 collective-permute-start.1
  501.2 27.1 %fwd_a4.1.refs_3_ = bf16[2048,768]{1,0:T(8,128)(2,1)} custom-call(bf16[4096,768]{1,0:T(8,128)(2,1)} %get-tuple-element.53.refs_0_, bf16[4,4,2,768,768]{4,3,2,1,0:T(8,128)(2,1)} %get-tuple-element.52.refs_1_), custom_call_target="tpu_custom_call" | custom-call | flops 19327352832 | bytes 15728640 | tf_op jit(solution)/shard_map/fwd_a4/pallas_call | solution.py:200
  528.3 0.5 collective-permute-start.3
  528.9 91.5 %fwd_b.1 = (bf16[16,2048,768]{2,1,0:T(8,128)(2,1)}, bf16[2048,768]{1,0:T(8,128)(2,1)}) custom-call(bf16[16,2048,768]{2,1,0:T(8,128)(2,1)} %refs_0_.5, bf16[4,4,2,768,768]{4,3,2,1,0:T(8,128)(2,1)} %get-tuple-element.52.refs_1_), custom_call_target="tpu_custom_call" | custom-call | flops 77309411328 | bytes 44040192 | tf_op jit(solution)/shard_map/fwd_b/pallas_call | solution.py:200
  620.4 1.2 slice.3
  621.6 1.3 pad_maximum_fusion.scal_ref
  622.9 2.0 collective-permute-start.5
  625.2 48.4 %fwd_c.1 = (bf16[16,2048,768]{2,1,0:T(8,128)(2,1)}, bf16[1024,768]{1,0:T(8,128)(2,1)}) custom-call(bf16[16,2048,768]{2,1,0:T(8,128)(2,1)} %refs_0_.5, bf16[4,4,2,768,768]{4,3,2,1,0:T(8,128)(2,1)} %get-tuple-element.52.refs_1_, bf16[2048,768]{1,0:T(8,128)(2,1)} %fwd_a3.1.refs_2_, bf16[2048,768]{1,0:T(8,128)(2,1)} %fwd_a4.1.refs_3_, ...), custom_call_target="tpu_custom_call", output_to_operand_aliasing={{0}: (6, {})} | custom-call | flops 38654705664 | bytes 40894464 | tf_op jit(solution)/shard_map/fwd_c/pallas_call | solution.py:200
  673.6 0.4 collective-permute-start.14
  674.2 48.7 %fwd_d.1 = (bf16[16,2048,768]{2,1,0:T(8,128)(2,1)}, bf16[1024,768]{1,0:T(8,128)(2,1)}) custom-call(bf16[16,2048,768]{2,1,0:T(8,128)(2,1)} %refs_0_.5, bf16[4,4,2,768,768]{4,3,2,1,0:T(8,128)(2,1)} %get-tuple-element.52.refs_1_, bf16[2048,768]{1,0:T(8,128)(2,1)} %collective-permute-done.1.refs_2_, ...), custom_call_target="tpu_custom_call", output_to_operand_aliasing={{0}: (5, {})} | custom-call | flops 38654705664 | bytes 40894464 | tf_op jit(solution)/shard_map/fwd_d/pallas_call | solution.py:200
  722.9 1.9 collective-permute-start.11
  724.8 27.6 %upd_second.1 = (f32[1,3072,768]{2,1,0:T(8,128)}, f32[1,3072,768]{2,1,0:T(8,128)}, f32[1,3072,768]{2,1,0:T(8,128)}) custom-call(f32[2]{0:T(128)} %pad_maximum_fusion.scal_ref, f32[4,768,768]{2,1,0:T(8,128)} %all-gather.3.cloned.1.call-done.g_ref, f32[1,3072,768]{2,1,0:T(8,128)} %w_ref.2, f32[1,3072,768]{2,1,0:T(8,128)} %m_ref.2, f32[1,3072,768]{2,1,0:T(8,128)} %v_ref.2), custom_call_target="tpu_custom_call" | custom-call | flops 20000000000 | bytes 66060288 | tf_op jit(solution)/shard_map/upd_second/pallas_call | solution.py:265
  752.4 0.2 collective-permute-start.8
  752.6 27.6 %upd_first.1 = (f32[1,768,3072]{2,1,0:T(8,128)}, f32[1,768,3072]{2,1,0:T(8,128)}, f32[1,768,3072]{2,1,0:T(8,128)}) custom-call(f32[2]{0:T(128)} %pad_maximum_fusion.scal_ref, f32[4,768,768]{2,1,0:T(8,128)} %all-gather.5.cloned.1.call-done.g_ref, f32[1,768,3072]{2,1,0:T(8,128)} %w_ref.3, f32[1,768,3072]{2,1,0:T(8,128)} %m_ref.3, f32[1,768,3072]{2,1,0:T(8,128)} %v_ref.3), custom_call_target="tpu_custom_call" | custom-call | flops 20000000000 | bytes 66060288 | tf_op jit(solution)/shard_map/upd_first/pallas_call | solution.py:265
  780.2 0.3 collective-permute-start.10
  780.6 0.2 collective-permute-start.12
  780.8 0.3 collective-permute-start.9
  781.1 8.7 %put_a.1.refs_6_ = bf16[16,2048,768]{2,1,0:T(8,128)(2,1)} custom-call(bf16[2048,768]{1,0:T(8,128)(2,1)} %collective-permute-done.refs_0_, bf16[2048,768]{1,0:T(8,128)(2,1)} %collective-permute-done.13.refs_1_, bf16[1024,768]{1,0:T(8,128)(2,1)} %collective-permute-done.14.refs_2_, ...), custom_call_target="tpu_custom_call", output_to_operand_aliasing={{}: (4, {})} | custom-call | flops 1651507200 | bytes 22020096 | tf_op jit(solution)/shard_map/put_a/pallas_call | solution.py:238
  789.9 8.4 %put_b.1 = bf16[16,2048,768]{2,1,0:T(8,128)(2,1)} custom-call(bf16[2048,768]{1,0:T(8,128)(2,1)} %collective-permute-done.8.refs_0_, bf16[1024,768]{1,0:T(8,128)(2,1)} %collective-permute-done.4.refs_1_, bf16[1024,768]{1,0:T(8,128)(2,1)} %collective-permute-done.9.refs_2_, ...), custom_call_target="tpu_custom_call", output_to_operand_aliasing={{}: (6, {})} | custom-call | flops 1651507200 | bytes 22020096 | tf_op jit(solution)/shard_map/put_b/pallas_call | solution.py:238
  (26 shorter events, 0.6 us)
Async XLA Ops:
  7.2 717.6 %all-gather.3.cloned.1.call-start = ((), (), s32[]{:S(2)}) async-start(), calls=%async_computation | async-start | bytes 11796480 | tf_op jit(solution)/shard_map/all_gather | solution.py:798
  467.5 285.1 %all-gather.5.cloned.1.call-start = ((), (), s32[]{:S(2)}) async-start(), calls=%async_computation.1 | async-start | bytes 11796480 | tf_op jit(solution)/shard_map/all_gather | solution.py:799
  494.9 128.0 %collective-permute-start.1 = (bf16[2048,768]{1,0:T(8,128)(2,1)}, bf16[2048,768]{1,0:T(8,128)(2,1)}, u32[]{:S(2)}, u32[]{:S(2)}) collective-permute-start(bf16[2048,768]{1,0:T(8,128)(2,1)} %fwd_a3.1.refs_2_), channel_id=1, source_target_pairs={{0,2},{1,3},{2,0},{3,1},{4,6},{5,7},{6,4},{7,5},{8,10},{9,11},{10,... | collective-permute-start | bytes 9437192 | tf_op jit(solution)/shard_map/ppermute | solution.py:784
  501.1 121.7 %collective-permute-start.2 = (bf16[2048,768]{1,0:T(8,128)(2,1)}, bf16[2048,768]{1,0:T(8,128)(2,1)}, u32[]{:S(2)}, u32[]{:S(2)}) collective-permute-start(bf16[2048,768]{1,0:T(8,128)(2,1)} %fwd_a3.1.refs_2_), channel_id=1, source_target_pairs={{0,1},{1,0},{2,3},{3,2},{4,5},{5,4},{6,7},{7,6},{8,9},{9,8},{10,11... | collective-permute-start | bytes 9437192 | tf_op jit(solution)/shard_map/ppermute | solution.py:781
  528.3 94.6 %collective-permute-start.3 = (bf16[2048,768]{1,0:T(8,128)(2,1)}, bf16[2048,768]{1,0:T(8,128)(2,1)}, u32[]{:S(2)}, u32[]{:S(2)}) collective-permute-start(bf16[2048,768]{1,0:T(8,128)(2,1)} %fwd_a4.1.refs_3_), channel_id=1, source_target_pairs={{0,1},{1,0},{2,3},{3,2},{4,5},{5,4},{6,7},{7,6},{8,9},{9,8},{10,11... | collective-permute-start | bytes 9437192 | tf_op jit(solution)/shard_map/ppermute | solution.py:781
  528.8 144.8 %collective-permute-start = (bf16[2048,768]{1,0:T(8,128)(2,1)}, bf16[2048,768]{1,0:T(8,128)(2,1)}, u32[]{:S(2)}, u32[]{:S(2)}) collective-permute-start(bf16[2048,768]{1,0:T(8,128)(2,1)} %fwd_a4.1.refs_3_), channel_id=1, source_target_pairs={{0,2},{1,3},{2,0},{3,1},{4,6},{5,7},{6,4},{7,5},{8,10},{9,11},{10,... | collective-permute-start | bytes 9437192 | tf_op jit(solution)/shard_map/ppermute | solution.py:784
  622.9 51.3 %collective-permute-start.7 = (bf16[2048,768]{1,0:T(8,128)(2,1)}, bf16[2048,768]{1,0:T(8,128)(2,1)}, u32[]{:S(2)}, u32[]{:S(2)}) collective-permute-start(bf16[2048,768]{1,0:T(8,128)(2,1)} %get-tuple-element.61), channel_id=1, source_target_pairs={{0,1},{1,0},{2,3},{3,2},{4,5},{5,4},{6,7},{7,6},{8,9},{9,8},{10,11... | collective-permute-start | bytes 9437192 | tf_op jit(solution)/shard_map/ppermute | solution.py:781
  622.9 129.4 %collective-permute-start.5 = (bf16[2048,768]{1,0:T(8,128)(2,1)}, bf16[2048,768]{1,0:T(8,128)(2,1)}, u32[]{:S(2)}, u32[]{:S(2)}) collective-permute-start(bf16[2048,768]{1,0:T(8,128)(2,1)} %get-tuple-element.61), channel_id=1, source_target_pairs={{0,2},{1,3},{2,0},{3,1},{4,6},{5,7},{6,4},{7,5},{8,10},{9,11},{10,... | collective-permute-start | bytes 9437192 | tf_op jit(solution)/shard_map/ppermute | solution.py:784
  625.0 49.1 %collective-permute-start.6 = (bf16[2048,768]{1,0:T(8,128)(2,1)}, bf16[2048,768]{1,0:T(8,128)(2,1)}, u32[]{:S(2)}, u32[]{:S(2)}) collective-permute-start(bf16[2048,768]{1,0:T(8,128)(2,1)} %collective-permute-done.1.refs_2_), channel_id=1, source_target_pairs={{0,1},{1,0},{2,3},{3,2},{4,5},{5,4},{6,7},{7,6},{8,9},{9,8},{10,11... | collective-permute-start | bytes 9437192 | tf_op jit(solution)/shard_map/ppermute | solution.py:781
  673.6 107.2 %collective-permute-start.14 = (bf16[1024,768]{1,0:T(8,128)(2,1)}, bf16[1024,768]{1,0:T(8,128)(2,1)}, u32[]{:S(2)}, u32[]{:S(2)}) collective-permute-start(bf16[1024,768]{1,0:T(8,128)(2,1)} %get-tuple-element.60), channel_id=1, source_target_pairs={{0,1},{1,0},{2,3},{3,2},{4,5},{5,4},{6,7},{7,6},{8,9},{9,8},{10,11... | collective-permute-start | bytes 4718600 | tf_op jit(solution)/shard_map/ppermute | solution.py:781
  674.0 106.2 %collective-permute-start.4 = (bf16[1024,768]{1,0:T(8,128)(2,1)}, bf16[1024,768]{1,0:T(8,128)(2,1)}, u32[]{:S(2)}, u32[]{:S(2)}) collective-permute-start(bf16[1024,768]{1,0:T(8,128)(2,1)} %get-tuple-element.60), channel_id=1, source_target_pairs={{0,2},{1,3},{2,0},{3,1},{4,6},{5,7},{6,4},{7,5},{8,10},{9,11},{10,... | collective-permute-start | bytes 4718600 | tf_op jit(solution)/shard_map/ppermute | solution.py:784
  674.0 107.0 %collective-permute-start.13 = (bf16[2048,768]{1,0:T(8,128)(2,1)}, bf16[2048,768]{1,0:T(8,128)(2,1)}, u32[]{:S(2)}, u32[]{:S(2)}) collective-permute-start(bf16[2048,768]{1,0:T(8,128)(2,1)} %collective-permute-done.refs_0_), channel_id=1, source_target_pairs={{0,1},{1,0},{2,3},{3,2},{4,5},{5,4},{6,7},{7,6},{8,9},{9,8},{10,11... | collective-permute-start | bytes 9437192 | tf_op jit(solution)/shard_map/ppermute | solution.py:781
  722.9 57.7 %collective-permute-start.11 = (bf16[1024,768]{1,0:T(8,128)(2,1)}, bf16[1024,768]{1,0:T(8,128)(2,1)}, u32[]{:S(2)}, u32[]{:S(2)}) collective-permute-start(bf16[1024,768]{1,0:T(8,128)(2,1)} %get-tuple-element.80), channel_id=1, source_target_pairs={{0,2},{1,3},{2,0},{3,1},{4,6},{5,7},{6,4},{7,5},{8,10},{9,11},{10,... | collective-permute-start | bytes 4718600 | tf_op jit(solution)/shard_map/ppermute | solution.py:784
  752.4 37.5 %collective-permute-start.8 = (bf16[2048,768]{1,0:T(8,128)(2,1)}, bf16[2048,768]{1,0:T(8,128)(2,1)}, u32[]{:S(2)}, u32[]{:S(2)}) collective-permute-start(bf16[2048,768]{1,0:T(8,128)(2,1)} %collective-permute-done.5.refs_3_), channel_id=1, source_target_pairs={{0,1},{1,0},{2,3},{3,2},{4,5},{5,4},{6,7},{7,6},{8,9},{9,8},{10,11... | collective-permute-start | bytes 9437192 | tf_op jit(solution)/shard_map/ppermute | solution.py:781
  780.2 9.6 %collective-permute-start.10 = (bf16[1024,768]{1,0:T(8,128)(2,1)}, bf16[1024,768]{1,0:T(8,128)(2,1)}, u32[]{:S(2)}, u32[]{:S(2)}) collective-permute-start(bf16[1024,768]{1,0:T(8,128)(2,1)} %get-tuple-element.80), channel_id=1, source_target_pairs={{0,1},{1,0},{2,3},{3,2},{4,5},{5,4},{6,7},{7,6},{8,9},{9,8},{10,11... | collective-permute-start | bytes 4718600 | tf_op jit(solution)/shard_map/ppermute | solution.py:781
  780.6 9.3 %collective-permute-start.12 = (bf16[1024,768]{1,0:T(8,128)(2,1)}, bf16[1024,768]{1,0:T(8,128)(2,1)}, u32[]{:S(2)}, u32[]{:S(2)}) collective-permute-start(bf16[1024,768]{1,0:T(8,128)(2,1)} %collective-permute-done.11.refs_4_), channel_id=1, source_target_pairs={{0,1},{1,0},{2,3},{3,2},{4,5},{5,4},{6,7},{7,6},{8,9},{9,8},{10,11... | collective-permute-start | bytes 4718600 | tf_op jit(solution)/shard_map/ppermute | solution.py:781
  780.8 9.1 %collective-permute-start.9 = (bf16[1024,768]{1,0:T(8,128)(2,1)}, bf16[1024,768]{1,0:T(8,128)(2,1)}, u32[]{:S(2)}, u32[]{:S(2)}) collective-permute-start(bf16[1024,768]{1,0:T(8,128)(2,1)} %collective-permute-done.4.refs_1_), channel_id=1, source_target_pairs={{0,1},{1,0},{2,3},{3,2},{4,5},{5,4},{6,7},{7,6},{8,9},{9,8},{10,11... | collective-permute-start | bytes 4718600 | tf_op jit(solution)/shard_map/ppermute | solution.py:781
Sparse Core Ops, SparseCore 0:
  467.6 98.0 all-gather.2
  567.6 92.3 all-gather.4

commit v3 on v2

--- a/solution.py
+++ b/solution.py
@@ -51,8 +51,8 @@
     scaled = clip_coef * grad_val
     mom_new = BETA_ONE * moment + (1.0 - BETA_ONE) * scaled
     sec_new = BETA_TWO * second + (1.0 - BETA_TWO) * scaled * scaled
-    mom_hat = mom_new / (1.0 - BETA_ONE ** STEP_COUNT)
-    sec_hat = sec_new / (1.0 - BETA_TWO ** STEP_COUNT)
+    mom_hat = mom_new * (1.0 / (1.0 - BETA_ONE ** STEP_COUNT))
+    sec_hat = sec_new * (1.0 / (1.0 - BETA_TWO ** STEP_COUNT))
     param_new = param_old - lr_value * (mom_hat / (jnp.sqrt(sec_hat) + ADAM_EPS) + WEIGHT_DECAY * param_old)
     return param_new, mom_new, sec_new
 
@@ -253,20 +253,21 @@
 
 
 def run_update(scal, grad, w, m, v, name):
-    rows = 192
+    rows = HALF
     _, n_row, n_col = w.shape
     per = n_row // rows
     if n_col == FFN:
         par = pl.BlockSpec((1, rows, DIM), lambda j, i: (0, i, j))
-        grid, g_spec = (4, 4), pl.BlockSpec((1, rows, DIM), lambda j, i: (j, i, 0))
+        grid, g_spec = (4, 2), pl.BlockSpec((1, rows, DIM), lambda j, i: (j, i, 0))
     else:
-        par = pl.BlockSpec((1, rows, DIM), lambda j, i: (0, 4 * j + i, 0))
-        grid, g_spec = (4, 4), pl.BlockSpec((1, rows, DIM), lambda j, i: (j, i, 0))
+        par = pl.BlockSpec((1, rows, DIM), lambda j, i: (0, 2 * j + i, 0))
+        grid, g_spec = (4, 2), pl.BlockSpec((1, rows, DIM), lambda j, i: (j, i, 0))
     return pl.pallas_call(
         update_kernel, grid=grid,
         in_specs=[pl.BlockSpec(memory_space=pltpu.SMEM), g_spec, par, par, par], out_specs=[par] * 3,
         out_shape=[jax.ShapeDtypeStruct(w.shape, F32)] * 3, name=name,
         cost_estimate=pl.CostEstimate(flops=20_000_000_000, bytes_accessed=7 * 9 * MIB, transcendentals=n_row * n_col),
+        compiler_params=pltpu.CompilerParams(vmem_limit_bytes=VMEM_BIG),
     )(scal, grad, w, m, v)
 
 
@@ -604,7 +605,7 @@
 
 
 def middle_kernel(lr_ref, mx_ref, r1_ref, r2_ref, w1_ref, m1_ref, v1_ref, w2_ref, m2_ref, v2_ref, x_ref,
-                  y_ref, all_ref, scal_ref, r_v, p_v, q_v, s_v, n_v, w_v, x_buf, h_buf,
+                  y0_ref, y1_ref, all_ref, scal_ref, r_v, p_v, q_v, s_v, n_v, w_v, x_buf, h_buf,
                   r_sem, p_sem, x_sem, ns, nr, hs, hr, xs, xr, o_sem, y_sem, *sems):
     stage, core, rep, mate, _ = ids()
     side = lax.div(stage, 2)
@@ -716,33 +717,42 @@
 
     def y_copy(t):
         rows = pl.ds(pl.multiple_of(t * TILE, TILE), TILE)
-        return pltpu.make_async_copy(x_buf.at[rows], y_ref.at[rows], y_sem.at[t])
+        return pltpu.make_async_copy(x_buf.at[rows], y0_ref.at[rows], y_sem.at[t])
+
+    y1_copy = pltpu.make_async_copy(x_buf.at[pl.ds(ROWS, ROWS)], y1_ref, y_sem.at[n_tile - 1])
 
     def blk_body(blk, _):
         keep(blk).start()
         steps = steps_of(blk + 1)
+        more = blk < 3
 
         def tile_body(t, _):
             for when, step in zip((0, 3, 5, 7), steps):
-                pl.when(t == when)(step)
-            mlp_tile(x_buf, pl.ds(pl.multiple_of(t * TILE, TILE), TILE), w_v.at[blk], h_buf)
-
-            @pl.when(jnp.logical_and(blk == 2, t > 0))
+                pl.when(jnp.logical_and(more, t == when))(step)
+            mlp_tile(x_buf, pl.ds(pl.multiple_of(t * TILE, TILE), TILE), w_v.at[lax.rem(blk, 3)], h_buf)
+
+            @pl.when(jnp.logical_and(blk == 3, t > 0))
             def _():
                 y_copy(t - 1).start()
             return 0
-        lax.fori_loop(0, n_tile, tile_body, 0)
-        for step in steps[4:]:
-            step()
+        lax.fori_loop(0, jnp.where(more, n_tile, n_tile // 2), tile_body, 0)
+
+        @pl.when(more)
+        def _():
+            for step in steps[4:]:
+                step()
+
+        @pl.when(blk == 2)
+        def _():
+            y1_copy.start()
         keep(blk).wait()
         return 0
 
-    lax.fori_loop(0, 3, blk_body, 0)
-    y_copy(n_tile - 1).start()
-    keep(3).start()
-    for t in range(n_tile):
+    lax.fori_loop(0, 4, blk_body, 0)
+    y_copy(n_tile // 2 - 1).start()
+    y1_copy.wait()
+    for t in range(n_tile // 2):
         y_copy(t).wait()
-    keep(3).wait()
 
 
 def run_middle(lr, mx, r1, r2, w1, m1, v1, w2, m2, v2, x):
@@ -750,8 +760,8 @@
     n_rows = 2 * ROWS
     return pl.pallas_call(
         middle_kernel, in_specs=[smem, smem] + [ANY] * 9,
-        out_specs=[ANY] * 2 + [pl.BlockSpec(memory_space=pltpu.VMEM)],
-        out_shape=[jax.ShapeDtypeStruct((n_rows, DIM), BF16), jax.ShapeDtypeStruct((4, 4, 2, DIM, DIM), BF16), jax.ShapeDtypeStruct((8, 128), F32)], name='middle',
+        out_specs=[ANY] * 3 + [pl.BlockSpec(memory_space=pltpu.VMEM)],
+        out_shape=[jax.ShapeDtypeStruct((ROWS, DIM), BF16)] * 2 + [jax.ShapeDtypeStruct((4, 4, 2, DIM, DIM), BF16), jax.ShapeDtypeStruct((8, 128), F32)], name='middle',
         scratch_shapes=[
             pltpu.VMEM((2, DIM, DIM), F32), pltpu.VMEM((2, 3, HALF, DIM), F32), pltpu.VMEM((4, 2, HALF, DIM), BF16),
             pltpu.VMEM((2, HALF, DIM), BF16), pltpu.VMEM((16, 8, 128), F32), pltpu.VMEM((3, 4, 2, DIM, DIM), BF16),
@@ -770,30 +780,29 @@
     def stage_program(w_in, w_out, mom_in, mom_out, var_in, var_out, acc_in, acc_out, stage_acts, d_out, next_x, learn_rate, max_norm):
         act_h, pre_keep, grad_keep = run_backward(stage_acts, d_out, w_in, w_out)
         sh_second, sh_first = run_reduce(act_h, grad_keep, stage_acts, pre_keep, acc_out, acc_in)
-        rows_a, weights, scal = run_middle(learn_rate, max_norm, sh_first, sh_second, w_in, mom_in, var_in, w_out, mom_out, var_out, next_x)
+        def to_mate(rows):
+            return lax.ppermute(rows, 'stage', CORE_PERM)
+
+        def to_far(rows):
+            return lax.ppermute(rows, 'stage', X_PERM)
+
+        y_0, rows_a, weights, scal = run_middle(learn_rate, max_norm, sh_first, sh_second, w_in, mom_in, var_in, w_out, mom_out, var_out, next_x)
         scal = jnp.stack([scal[0, 0], learn_rate[0]])
         sh_second, sh_first, rows_a = lax.optimization_barrier((sh_second, sh_first, rows_a))
-        y_0 = run_forward(rows_a, weights, CHUNK_0, 'fwd_a3', blocks=(3,))
-        rows_a, y_0 = lax.optimization_barrier((rows_a, y_0))
-        y_1 = run_forward(rows_a, weights, CHUNK_0[:1] + (ROWS, ROWS), 'fwd_a4', blocks=(3,))
-
-        def to_mate(rows):
-            return lax.ppermute(rows, 'stage', CORE_PERM)
-
-        def to_far(rows):
-            return lax.ppermute(rows, 'stage', X_PERM)
-
-        far_0, far_1, mate_0, mate_1 = to_far(y_0), to_far(y_1), to_mate(y_0), to_mate(y_1)
-        out, y_2 = run_forward(next_x, weights, CHUNK_2, 'fwd_b', to_out=True)
-        far_0, mate_0, mate_1, y_2 = lax.optimization_barrier((far_0, mate_0, mate_1, y_2))
+        far_0, mate_0 = to_far(y_0), to_mate(y_0)
+        y_1 = run_forward(rows_a, weights, CHUNK_0, 'fwd_a3', blocks=(3,))
+        far_1, mate_1 = to_far(y_1), to_mate(y_1)
+        sides = [(y_0, OWN, CHUNK_0), (y_1, OWN, CHUNK_1), (mate_0, MATE, CHUNK_0)]
+        out, y_2 = run_forward(next_x, weights, CHUNK_2, 'fwd_b', to_out=True, sides=sides)
+        far_0, mate_1, y_2 = lax.optimization_barrier((far_0, mate_1, y_2))
         relay_0 = to_mate(far_0)
         far_2, mate_2 = to_far(y_2), to_mate(y_2)
-        sides = [(y_0, OWN, CHUNK_0), (y_1, OWN, CHUNK_1), (mate_0, MATE, CHUNK_0), (mate_1, MATE, CHUNK_1)]
+        sides = [(mate_1, MATE, CHUNK_1), (far_0, FAR, CHUNK_0)]
         out, y_3 = run_forward(next_x, weights, CHUNK_3, 'fwd_c', to_out=True, out_buf=out, sides=sides)
         far_1, y_3 = lax.optimization_barrier((far_1, y_3))
         relay_1 = to_mate(far_1)
         far_3, mate_3 = to_far(y_3), to_mate(y_3)
-        sides = [(far_0, FAR, CHUNK_0), (relay_0, RELAY, CHUNK_0), (mate_2, MATE, CHUNK_2)]
+        sides = [(far_1, FAR, CHUNK_1), (relay_0, RELAY, CHUNK_0), (mate_2, MATE, CHUNK_2)]
         out, y_4 = run_forward(next_x, weights, CHUNK_4, 'fwd_d', to_out=True, out_buf=out, sides=sides)
         full_second = lax.all_gather(sh_second[0], 'data')
         full_first = lax.all_gather(sh_first[0], 'data')
@@ -805,7 +814,7 @@
         new_first, mom_first, sec_first = run_update(scal, full_first, w_in, mom_in, var_in, 'upd_first')
         far_3, new_first = lax.optimization_barrier((far_3, new_first))
         relay_3, relay_4 = to_mate(far_3), to_mate(far_4)
-        out = run_copy(out, [(far_1, FAR, CHUNK_1), (relay_1, RELAY, CHUNK_1), (mate_3, MATE, CHUNK_3), (far_2, FAR, CHUNK_2)], 'put_a')
+        out = run_copy(out, [(relay_1, RELAY, CHUNK_1), (mate_3, MATE, CHUNK_3), (far_2, FAR, CHUNK_2)], 'put_a')
         out = run_copy(out, [(relay_2, RELAY, CHUNK_2), (far_3, FAR, CHUNK_3), (relay_3, RELAY, CHUNK_3), (mate_4, MATE, CHUNK_4), (far_4, FAR, CHUNK_4), (relay_4, RELAY, CHUNK_4)], 'put_b')
         return (new_first, new_second, mom_first, mom_second, sec_first, sec_second, out)
 

time: 812 us -> 792 us (0.975)
  Pallas kernels: 774 us -> 754 us
    pallas_call x5 -> x4, Pallas kernels: 243 us -> 215 us  [run_forward(): pl.pallas_call(functools.partial(forward_kernel, tuple(blocks), spec, len...]
    pallas_call x1, Pallas kernels: 215 us -> 233 us  [run_middle(): pl.pallas_call(middle_kernel, in_specs=[smem, smem] + [ANY] * 9, out_spec...]
  transfers between devices with their start and end apart: 17 -> 17, of which waited for: 0 -> 1; matrix products, arithmetic and copies ran while one was open for 0% -> 0% of each run, Pallas kernels for 38% -> 34%
where the time goes in v3:
time: 792 us; the launch traced here: 787 us
  Pallas kernels  754 us (95%)
  between operations  15.9 us (2%)
  starting transfers between devices  12.7 us (2%)
    pallas_call x1, Pallas kernels, run_middle(): pl.pallas_call(middle_kernel, in_specs=[smem, smem] + [ANY] * 9, out_spec...  233 us
    pallas_call x4, Pallas kernels, run_forward(): pl.pallas_call(functools.partial(forward_kernel, tuple(blocks), spec, len...  215 us
    pallas_call x1, Pallas kernels, run_reduce(): pl.pallas_call(reduce_kernel, in_specs=[ANY] * 6, out_specs=[ANY] * 2, ou...  166 us
    pallas_call x1, Pallas kernels, run_backward(): pl.pallas_call(backward_kernel, in_specs=[ANY] * 4, out_specs=[ANY] * 3,...  77.6 us
    pallas_call x2, Pallas kernels, run_update(): pl.pallas_call(update_kernel, grid=grid, in_specs=[pl.BlockSpec(memory_sp...  47.9 us
  transfers between devices with their start and end apart: 17, of which 1 were waited for; matrix products, arithmetic and copies ran while one was open for 0% of the time, Pallas kernels for 34%

profile of v3, /device:TPU:0, one launch (start us, length us, event | category | flops | bytes accessed | tf_op | source)
XLA Modules:
  0.0 786.6 jit_solution(4155451449338576172)
XLA Ops:
  8.5 77.6 %backward.1 = (bf16[2048,3072]{1,0:T(8,128)(2,1)}, bf16[2048,3072]{1,0:T(8,128)(2,1)}, bf16[2048,768]{1,0:T(8,128)(2,1)}) custom-call(bf16[1,2048,768]{2,1,0:T(8,128)(2,1)} %a_ref.3, bf16[2048,768]{1,0:T(8,128)(2,1)} %d_ref.1, f32[1,768,3072]{2,1,0:T(8,128)} %w_ref.3, f32[1,3072,768]{2,1,0:T(8,128)} %w_ref.2), custom_call_target="tpu_custom_call" | custom-call | flops 28991029248 | bytes 50000000 | tf_op jit(solution)/shard_map/backward/pallas_call | solution.py:593
  86.1 166.3 %reduce.1 = (f32[1,768,768]{2,1,0:T(8,128)}, f32[1,768,768]{2,1,0:T(8,128)}) custom-call(bf16[2048,3072]{1,0:T(8,128)(2,1)} %get-tuple-element.43.h_ref, bf16[2048,768]{1,0:T(8,128)(2,1)} %get-tuple-element.44.g_ref, bf16[1,2048,768]{2,1,0:T(8,128)(2,1)} %a_ref.3, bf16[2048,3072]{1,0:T(8,128)(2,1)} %get-tuple-element.45.p_ref, f32[1,1,3072,768]{3,2,1,0:T(8,128)} %acc2_ref.1, ...), custom_call_target="tpu_custom_call" | custom-call | flops 149999992832 | bytes 73400320 | tf_op jit(solution)/shard_map/reduce/pallas_call | solution.py:458
  252.5 232.7 %middle.1 = (bf16[2048,768]{1,0:T(8,128)(2,1)}, bf16[2048,768]{1,0:T(8,128)(2,1)}, bf16[4,4,2,768,768]{4,3,2,1,0:T(8,128)(2,1)}, f32[8,128]{1,0:T(8,128)}) custom-call(f32[1]{0:T(128)S(6)} %copy.28.lr_ref, f32[1]{0:T(128)S(6)} %copy.29.mx_ref, f32[1,768,768]{2,1,0:T(8,128)} %get-tuple-element.67.r1_ref, f32[1,768,768]{2,1,0:T(8,128)} %get-tuple-element.64.r2_ref, ...), custom_call_target="tpu_custom_call" | custom-call | flops 199999995904 | bytes 104857600 | tf_op jit(solution)/shard_map/middle/pallas_call | solution.py:761
  485.2 0.3 all-gather.5.cloned.1.call-start
  485.5 6.2 collective-permute-start.1
  491.7 27.1 %fwd_a3.1.refs_3_ = bf16[2048,768]{1,0:T(8,128)(2,1)} custom-call(bf16[2048,768]{1,0:T(8,128)(2,1)} %get-tuple-element.49.refs_0_, bf16[4,4,2,768,768]{4,3,2,1,0:T(8,128)(2,1)} %get-tuple-element.50.refs_1_), custom_call_target="tpu_custom_call" | custom-call | flops 19327352832 | bytes 15728640 | tf_op jit(solution)/shard_map/fwd_a3/pallas_call | solution.py:200
  519.0 0.3 collective-permute-start
  519.3 1.2 slice.3
  520.5 1.3 pad_maximum_fusion.scal_ref
  521.8 91.4 %fwd_b.1 = (bf16[16,2048,768]{2,1,0:T(8,128)(2,1)}, bf16[2048,768]{1,0:T(8,128)(2,1)}) custom-call(bf16[16,2048,768]{2,1,0:T(8,128)(2,1)} %refs_0_.5, bf16[4,4,2,768,768]{4,3,2,1,0:T(8,128)(2,1)} %get-tuple-element.50.refs_1_, bf16[2048,768]{1,0:T(8,128)(2,1)} %get-tuple-element.51.refs_2_, bf16[2048,768]{1,0:T(8,128)(2,1)} %fwd_a3.1.refs_3_, ...), custom_call_target="tpu_custom_call" | custom-call | flops 77309411328 | bytes 44040192 | tf_op jit(solution)/shard_map/fwd_b/pallas_call | solution.py:200
  613.3 1.8 collective-permute-start.5
  615.3 48.6 %fwd_c.1 = (bf16[16,2048,768]{2,1,0:T(8,128)(2,1)}, bf16[1024,768]{1,0:T(8,128)(2,1)}) custom-call(bf16[16,2048,768]{2,1,0:T(8,128)(2,1)} %refs_0_.5, bf16[4,4,2,768,768]{4,3,2,1,0:T(8,128)(2,1)} %get-tuple-element.50.refs_1_, bf16[2048,768]{1,0:T(8,128)(2,1)} %collective-permute-done.2.refs_2_, ...), custom_call_target="tpu_custom_call", output_to_operand_aliasing={{0}: (4, {})} | custom-call | flops 38654705664 | bytes 40894464 | tf_op jit(solution)/shard_map/fwd_c/pallas_call | solution.py:200
  663.9 0.4 collective-permute-start.14
  664.3 0.2 collective-permute-start.4
  664.6 48.4 %fwd_d.1 = (bf16[16,2048,768]{2,1,0:T(8,128)(2,1)}, bf16[1024,768]{1,0:T(8,128)(2,1)}) custom-call(bf16[16,2048,768]{2,1,0:T(8,128)(2,1)} %refs_0_.5, bf16[4,4,2,768,768]{4,3,2,1,0:T(8,128)(2,1)} %get-tuple-element.50.refs_1_, bf16[2048,768]{1,0:T(8,128)(2,1)} %collective-permute-done.refs_2_, ...), custom_call_target="tpu_custom_call", output_to_operand_aliasing={{0}: (5, {})} | custom-call | flops 38654705664 | bytes 40894464 | tf_op jit(solution)/shard_map/fwd_d/pallas_call | solution.py:200
  713.0 1.8 collective-permute-start.11
  714.8 23.9 %upd_second.1 = (f32[1,3072,768]{2,1,0:T(8,128)}, f32[1,3072,768]{2,1,0:T(8,128)}, f32[1,3072,768]{2,1,0:T(8,128)}) custom-call(f32[2]{0:T(128)} %pad_maximum_fusion.scal_ref, f32[4,768,768]{2,1,0:T(8,128)} %all-gather.3.cloned.1.call-done.g_ref, f32[1,3072,768]{2,1,0:T(8,128)} %w_ref.2, f32[1,3072,768]{2,1,0:T(8,128)} %m_ref.2, f32[1,3072,768]{2,1,0:T(8,128)} %v_ref.2), custom_call_target="tpu_custom_call" | custom-call | flops 20000000000 | bytes 66060288 | tf_op jit(solution)/shard_map/upd_second/pallas_call | solution.py:265
  738.7 0.3 collective-permute-start.8
  739.0 24.0 %upd_first.1 = (f32[1,768,3072]{2,1,0:T(8,128)}, f32[1,768,3072]{2,1,0:T(8,128)}, f32[1,768,3072]{2,1,0:T(8,128)}) custom-call(f32[2]{0:T(128)} %pad_maximum_fusion.scal_ref, f32[4,768,768]{2,1,0:T(8,128)} %all-gather.5.cloned.1.call-done.g_ref, f32[1,768,3072]{2,1,0:T(8,128)} %w_ref.3, f32[1,768,3072]{2,1,0:T(8,128)} %m_ref.3, f32[1,768,3072]{2,1,0:T(8,128)} %v_ref.3), custom_call_target="tpu_custom_call" | custom-call | flops 20000000000 | bytes 66060288 | tf_op jit(solution)/shard_map/upd_first/pallas_call | solution.py:265
  763.0 0.3 collective-permute-start.10
  763.5 0.3 collective-permute-start.9
  763.8 6.1 put_a.1.refs_6_
  769.9 1.0 collective-permute-done.9.refs_2_
  770.9 8.4 %put_b.1 = bf16[16,2048,768]{2,1,0:T(8,128)(2,1)} custom-call(bf16[2048,768]{1,0:T(8,128)(2,1)} %collective-permute-done.8.refs_0_, bf16[1024,768]{1,0:T(8,128)(2,1)} %collective-permute-done.4.refs_1_, bf16[1024,768]{1,0:T(8,128)(2,1)} %collective-permute-done.9.refs_2_, ...), custom_call_target="tpu_custom_call", output_to_operand_aliasing={{}: (6, {})} | custom-call | flops 1651507200 | bytes 22020096 | tf_op jit(solution)/shard_map/put_b/pallas_call | solution.py:238
  (25 shorter events, 0.9 us)
Async XLA Ops:
  7.2 707.6 %all-gather.3.cloned.1.call-start = ((), (), s32[]{:S(2)}) async-start(), calls=%async_computation | async-start | bytes 11796480 | tf_op jit(solution)/shard_map/all_gather | solution.py:807
  485.2 253.8 %all-gather.5.cloned.1.call-start = ((), (), s32[]{:S(2)}) async-start(), calls=%async_computation.1 | async-start | bytes 11796480 | tf_op jit(solution)/shard_map/all_gather | solution.py:808
  485.4 36.4 %collective-permute-start.3 = (bf16[2048,768]{1,0:T(8,128)(2,1)}, bf16[2048,768]{1,0:T(8,128)(2,1)}, u32[]{:S(2)}, u32[]{:S(2)}) collective-permute-start(bf16[2048,768]{1,0:T(8,128)(2,1)} %get-tuple-element.51.refs_2_), channel_id=1, source_target_pairs={{0,1},{1,0},{2,3},{3,2},{4,5},{5,4},{6,7},{7,6},{8,9},{9,8},{10,11... | collective-permute-start | bytes 9437192 | tf_op jit(solution)/shard_map/ppermute | solution.py:784
  485.5 127.7 %collective-permute-start.1 = (bf16[2048,768]{1,0:T(8,128)(2,1)}, bf16[2048,768]{1,0:T(8,128)(2,1)}, u32[]{:S(2)}, u32[]{:S(2)}) collective-permute-start(bf16[2048,768]{1,0:T(8,128)(2,1)} %get-tuple-element.51.refs_2_), channel_id=1, source_target_pairs={{0,2},{1,3},{2,0},{3,1},{4,6},{5,7},{6,4},{7,5},{8,10},{9,11},{10,... | collective-permute-start | bytes 9437192 | tf_op jit(solution)/shard_map/ppermute | solution.py:787
  518.8 94.4 %collective-permute-start.2 = (bf16[2048,768]{1,0:T(8,128)(2,1)}, bf16[2048,768]{1,0:T(8,128)(2,1)}, u32[]{:S(2)}, u32[]{:S(2)}) collective-permute-start(bf16[2048,768]{1,0:T(8,128)(2,1)} %fwd_a3.1.refs_3_), channel_id=1, source_target_pairs={{0,1},{1,0},{2,3},{3,2},{4,5},{5,4},{6,7},{7,6},{8,9},{9,8},{10,11... | collective-permute-start | bytes 9437192 | tf_op jit(solution)/shard_map/ppermute | solution.py:784
  519.0 144.9 %collective-permute-start = (bf16[2048,768]{1,0:T(8,128)(2,1)}, bf16[2048,768]{1,0:T(8,128)(2,1)}, u32[]{:S(2)}, u32[]{:S(2)}) collective-permute-start(bf16[2048,768]{1,0:T(8,128)(2,1)} %fwd_a3.1.refs_3_), channel_id=1, source_target_pairs={{0,2},{1,3},{2,0},{3,1},{4,6},{5,7},{6,4},{7,5},{8,10},{9,11},{10,... | collective-permute-start | bytes 9437192 | tf_op jit(solution)/shard_map/ppermute | solution.py:787
  613.2 51.3 %collective-permute-start.7 = (bf16[2048,768]{1,0:T(8,128)(2,1)}, bf16[2048,768]{1,0:T(8,128)(2,1)}, u32[]{:S(2)}, u32[]{:S(2)}) collective-permute-start(bf16[2048,768]{1,0:T(8,128)(2,1)} %get-tuple-element.58), channel_id=1, source_target_pairs={{0,1},{1,0},{2,3},{3,2},{4,5},{5,4},{6,7},{7,6},{8,9},{9,8},{10,11... | collective-permute-start | bytes 9437192 | tf_op jit(solution)/shard_map/ppermute | solution.py:784
  613.3 125.4 %collective-permute-start.5 = (bf16[2048,768]{1,0:T(8,128)(2,1)}, bf16[2048,768]{1,0:T(8,128)(2,1)}, u32[]{:S(2)}, u32[]{:S(2)}) collective-permute-start(bf16[2048,768]{1,0:T(8,128)(2,1)} %get-tuple-element.58), channel_id=1, source_target_pairs={{0,2},{1,3},{2,0},{3,1},{4,6},{5,7},{6,4},{7,5},{8,10},{9,11},{10,... | collective-permute-start | bytes 9437192 | tf_op jit(solution)/shard_map/ppermute | solution.py:787
  615.1 49.4 %collective-permute-start.6 = (bf16[2048,768]{1,0:T(8,128)(2,1)}, bf16[2048,768]{1,0:T(8,128)(2,1)}, u32[]{:S(2)}, u32[]{:S(2)}) collective-permute-start(bf16[2048,768]{1,0:T(8,128)(2,1)} %collective-permute-done.1.refs_3_), channel_id=1, source_target_pairs={{0,1},{1,0},{2,3},{3,2},{4,5},{5,4},{6,7},{7,6},{8,9},{9,8},{10,11... | collective-permute-start | bytes 9437192 | tf_op jit(solution)/shard_map/ppermute | solution.py:784
  663.9 99.6 %collective-permute-start.14 = (bf16[1024,768]{1,0:T(8,128)(2,1)}, bf16[1024,768]{1,0:T(8,128)(2,1)}, u32[]{:S(2)}, u32[]{:S(2)}) collective-permute-start(bf16[1024,768]{1,0:T(8,128)(2,1)} %get-tuple-element.57), channel_id=1, source_target_pairs={{0,1},{1,0},{2,3},{3,2},{4,5},{5,4},{6,7},{7,6},{8,9},{9,8},{10,11... | collective-permute-start | bytes 4718600 | tf_op jit(solution)/shard_map/ppermute | solution.py:784
  664.3 98.6 %collective-permute-start.4 = (bf16[1024,768]{1,0:T(8,128)(2,1)}, bf16[1024,768]{1,0:T(8,128)(2,1)}, u32[]{:S(2)}, u32[]{:S(2)}) collective-permute-start(bf16[1024,768]{1,0:T(8,128)(2,1)} %get-tuple-element.57), channel_id=1, source_target_pairs={{0,2},{1,3},{2,0},{3,1},{4,6},{5,7},{6,4},{7,5},{8,10},{9,11},{10,... | collective-permute-start | bytes 4718600 | tf_op jit(solution)/shard_map/ppermute | solution.py:787
  664.6 99.2 %collective-permute-start.13 = (bf16[2048,768]{1,0:T(8,128)(2,1)}, bf16[2048,768]{1,0:T(8,128)(2,1)}, u32[]{:S(2)}, u32[]{:S(2)}) collective-permute-start(bf16[2048,768]{1,0:T(8,128)(2,1)} %collective-permute-done.refs_2_), channel_id=1, source_target_pairs={{0,1},{1,0},{2,3},{3,2},{4,5},{5,4},{6,7},{7,6},{8,9},{9,8},{10,11... | collective-permute-start | bytes 9437192 | tf_op jit(solution)/shard_map/ppermute | solution.py:784
  713.0 50.3 %collective-permute-start.11 = (bf16[1024,768]{1,0:T(8,128)(2,1)}, bf16[1024,768]{1,0:T(8,128)(2,1)}, u32[]{:S(2)}, u32[]{:S(2)}) collective-permute-start(bf16[1024,768]{1,0:T(8,128)(2,1)} %get-tuple-element.77), channel_id=1, source_target_pairs={{0,2},{1,3},{2,0},{3,1},{4,6},{5,7},{6,4},{7,5},{8,10},{9,11},{10,... | collective-permute-start | bytes 4718600 | tf_op jit(solution)/shard_map/ppermute | solution.py:787
  738.7 32.1 %collective-permute-start.8 = (bf16[2048,768]{1,0:T(8,128)(2,1)}, bf16[2048,768]{1,0:T(8,128)(2,1)}, u32[]{:S(2)}, u32[]{:S(2)}) collective-permute-start(bf16[2048,768]{1,0:T(8,128)(2,1)} %collective-permute-done.5.refs_2_), channel_id=1, source_target_pairs={{0,1},{1,0},{2,3},{3,2},{4,5},{5,4},{6,7},{7,6},{8,9},{9,8},{10,11... | collective-permute-start | bytes 9437192 | tf_op jit(solution)/shard_map/ppermute | solution.py:784
  763.0 6.9 collective-permute-start.10
  763.3 6.6 collective-permute-start.12
  763.5 7.3 collective-permute-start.9
Sparse Core Ops, SparseCore 0:
  485.3 98.1 all-gather.2
  585.3 92.3 all-gather.4
